TPU v7x, 32 devices: a 4x4x1 block of a 4x4x8 slice. The times are simulated.
32 devices in a mesh: layer: 1 (over z), col: 4 (over y), row: 8 (over x, core).
Axes of the slice: x: 4, y: 4, z: 1, core: 2. Of those that a mesh axis runs over, the one named last changes fastest.
The devices are a block of a 4x4x8 slice.
Arguments:
- weight: float32 [1280, 5120], P(('layer', 'row'), 'col')
- grad_in: float32 [1280, 5120], P(('layer', 'row'), 'col')
- mom_first: float32 [1280, 5120], P(('layer', 'row'), 'col')
- mom_second: float32 [1280, 5120], P(('layer', 'row'), 'col')
- stat_left: float32 [1280, 1280], P(('layer', 'row'), 'col')
- stat_right: float32 [5120, 5120], P(('layer', 'row'), 'col')
- basis_left: float32 [1280, 1280], P(('layer', 'row'), 'col')
- basis_right: float32 [5120, 5120], P(('layer', 'row'), 'col')
Outputs:
- output 1: float32 [1280, 5120], P(('layer', 'row'), 'col')
- output 2: float32 [1280, 5120], P(('layer', 'row'), 'col')
- output 3: float32 [1280, 5120], P(('layer', 'row'), 'col')
- output 4: float32 [1280, 1280], P(('layer', 'row'), 'col')
- output 5: float32 [5120, 5120], P(('layer', 'row'), 'col')
All inputs are finite; a program needn't handle non-finite values.
Results may differ from a plain program's by a relative error of at most 0.001.
Values are sent between devices in bfloat16 or wider.
A program may use at most 768 MiB of HBM per device.

v0:
```python
import jax
import jax.numpy as jnp
from jax import lax
from jax.sharding import PartitionSpec as P

BETA1 = 0.9
BETA2 = 0.9
EPS = 1e-8
LR = 0.1
STEP = 10
BIAS_ONE = 1.0 - BETA1 ** STEP
BIAS_TWO = 1.0 - BETA2 ** STEP


def solution(mesh):
    tile_spec = P(("layer", "row"), "col")
    highest = lax.Precision.HIGHEST
    contract_rows = (((0,), (0,)), ((), ()))
    contract_cols = (((1,), (1,)), ((), ()))

    def local_step(weight, grad_in, mom_first, mom_second, stat_left, stat_right, basis_left, basis_right):
        grad_rows = lax.all_gather(grad_in, "col", axis=1, tiled=True)
        grad_cols = lax.all_gather(grad_in, "row", axis=0, tiled=True)
        left_part = lax.dot_general(grad_in, grad_cols, contract_cols, precision=highest, preferred_element_type=jnp.float32)
        left_sum = lax.psum_scatter(left_part, "col", scatter_dimension=1, tiled=True)
        right_part = lax.dot_general(grad_rows, grad_in, contract_rows, precision=highest, preferred_element_type=jnp.float32)
        right_sum = lax.psum_scatter(right_part, "row", scatter_dimension=0, tiled=True)
        new_left = BETA2 * stat_left + (1.0 - BETA2) * left_sum
        new_right = BETA2 * stat_right + (1.0 - BETA2) * right_sum
        left_rows = lax.all_gather(basis_left.astype(jnp.bfloat16), "col", axis=1, tiled=True)
        right_cols = lax.all_gather(basis_right.astype(jnp.bfloat16), "row", axis=0, tiled=True)
        inner_rot = jnp.dot(grad_rows.astype(jnp.bfloat16), right_cols, preferred_element_type=jnp.float32).astype(jnp.bfloat16)
        rotated_part = lax.dot_general(left_rows, inner_rot, contract_rows, preferred_element_type=jnp.float32)
        rotated = lax.psum_scatter(rotated_part, "row", scatter_dimension=0, tiled=True)
        new_first = BETA1 * mom_first + (1.0 - BETA1) * rotated
        new_second = BETA2 * mom_second + (1.0 - BETA2) * rotated * rotated
        direction = (new_first / BIAS_ONE) / (jnp.sqrt(new_second / BIAS_TWO) + EPS)
        direction_cols = lax.all_gather(direction.astype(jnp.bfloat16), "row", axis=0, tiled=True)
        back_inner = jnp.dot(left_rows, direction_cols, preferred_element_type=jnp.float32).astype(jnp.bfloat16)
        update_part = lax.dot_general(back_inner, right_cols, contract_cols, preferred_element_type=jnp.float32)
        step_update = lax.psum_scatter(update_part, "col", scatter_dimension=1, tiled=True)
        new_weight = weight - LR * step_update
        return new_weight, new_first, new_second, new_left, new_right

    return jax.shard_map(local_step, mesh=mesh, in_specs=(tile_spec,) * 8, out_specs=(tile_spec,) * 5, check_vma=False)
```

profile of v0, /device:TPU:97, one launch (start us, length us, event | category | flops | bytes accessed | tf_op | source)
XLA Modules:
  0.0 462.5 jit_solution(14217519312892859898)
XLA Ops:
  7.2 0.1 all-gather.6.cloned.1.call-start
  7.2 0.7 all-gather.6.cloned.1.call-update
  8.0 0.1 all-gather.8.cloned.1.call-start
  8.1 3.3 convert_element_type.20
  11.4 0.1 reduce-scatter.13.cloned.1.call-start
  11.5 14.0 %all-gather = bf16[4,320,160]{1,2,0:T(8,128)(2,1)S(1)} all-gather(bf16[1,320,160]{1,2,0:T(8,128)(2,1)S(1)} %convert_bitcast_fusion), channel_id=1, replica_groups=mesh['layer'=1,'col'=4,'row'=8] {'col'}, dimensions={0}, use_global_device_ids=true | all-gather | bytes 512000 | tf_op jit(solution)/shard_map/all_gather | solution.py:30
  25.5 0.3 copy.28
  25.8 0.4 reshape.11
  26.1 26.4 %all-gather.6.cloned.1.call-done = f32[160,5120]{1,0:T(8,128)} async-done(((f32[160,1280]{1,0:T(8,128)}), f32[160,5120]{1,0:T(8,128)}) %all-gather.6.cloned.1.call-update) | async-done | bytes 3276816 | tf_op jit(solution)/shard_map/all_gather | solution.py:22
  52.6 69.5 %all-gather.8.cloned.1.call-done = bf16[5120,1280]{1,0:T(8,128)(2,1)} async-done(((bf16[640,1280]{1,0:T(8,128)(2,1)}), bf16[5120,1280]{1,0:T(8,128)(2,1)}) %all-gather.8.cloned.1.call-update) | async-done | bytes 13107216 | tf_op jit(solution)/shard_map/all_gather | solution.py:31
  122.1 12.4 %convolution_bitcast_fusion = f32[1280,1280]{0,1:T(8,128)} fusion(bf16[1280,160]{0,1:T(8,128)(2,1)S(1)} %reshape.11, bf16[5120,1280]{1,0:T(8,128)(2,1)} %all-gather.8.cloned.1.call-done, f32[160,5120]{1,0:T(8,128)} %all-gather.6.cloned.1.call-done), kind=kOutput, calls=%fused_computation | convolution fusion | flops 2622464000 | bytes 23347200 | tf_op jit(solution)/shard_map/dot_general | solution.py:33
  134.5 8.2 %copy.31 = f32[1280,1280]{1,0:T(8,128)} copy(f32[1280,1280]{0,1:T(8,128)} %convolution_bitcast_fusion) | data formatting | bytes 13107200
  142.7 0.1 all-gather.12.cloned.1.call-start
  142.8 0.6 all-gather.12.cloned.1.call-update
  143.4 0.1 all-gather.10.cloned.1.call-start
  143.5 40.2 %reduce-scatter.13.cloned.1.call-done = f32[160,1280]{1,0:T(8,128)} async-done(((f32[1280,1280]{1,0:T(8,128)}), f32[160,1280]{1,0:T(8,128)}) %reduce-scatter.13.cloned.1.call-update) | async-done | bytes 819216 | tf_op jit(solution)/shard_map/reduce_scatter | solution.py:34
  183.6 2.8 divide_convert_fusion
  186.5 0.1 reduce-scatter.15.cloned.1.call-start
  186.6 38.3 %all-gather.12.cloned.1.call-done = f32[1280,1280]{1,0:T(8,128)} async-done(((f32[160,1280]{1,0:T(8,128)}), f32[1280,1280]{1,0:T(8,128)}) %all-gather.12.cloned.1.call-update) | async-done | bytes 6553616 | tf_op jit(solution)/shard_map/all_gather | solution.py:23
  224.8 8.2 %convolution_bitcast_fusion.1 = f32[1280,160]{1,0:T(8,128)} fusion(f32[160,1280]{1,0:T(8,128)S(1)} %copy-done.1, f32[1280,1280]{1,0:T(8,128)} %all-gather.12.cloned.1.call-done), kind=kOutput, calls=%fused_computation.2 | convolution fusion | flops 3145728000 | bytes 8192000
  233.1 0.2 reduce-scatter.9.cloned.1.call-start
  233.3 19.1 %all-gather.10.cloned.1.call-done = bf16[1280,1280]{1,0:T(8,128)(2,1)} async-done(((bf16[160,1280]{1,0:T(8,128)(2,1)}), bf16[1280,1280]{1,0:T(8,128)(2,1)}) %all-gather.10.cloned.1.call-update) | async-done | bytes 3276816 | tf_op jit(solution)/shard_map/all_gather | solution.py:38
  252.5 12.4 %fusion.4 = f32[160,5120]{1,0:T(8,128)} fusion(bf16[5120,1280]{1,0:T(8,128)(2,1)} %all-gather.8.cloned.1.call-done, bf16[1280,160]{0,1:T(8,128)(2,1)S(1)} %reshape.11, bf16[1280,1280]{1,0:T(8,128)(2,1)} %all-gather.10.cloned.1.call-done), kind=kOutput, calls=%fused_computation.11 | convolution fusion | flops 2621644800 | bytes 20070400 | tf_op jit(solution)/shard_map/dot_general | solution.py:40
  264.9 0.1 reduce-scatter.11.cloned.1.call-start
  265.0 1.8 copy-done
  266.8 25.9 %fusion.6 = f32[5120,1280]{1,0:T(8,128)} fusion(f32[160,5120]{1,0:T(8,128)S(1)} %copy-done, f32[160,1280]{1,0:T(8,128)} %param.9), kind=kOutput, calls=%fused_computation.14 | convolution fusion | flops 12582912000 | bytes 30310400 | tf_op jit(solution)/shard_map/dot_general | solution.py:26
  292.8 1.3 copy.34
  294.0 1.7 multiply_add_fusion.2
  295.7 20.0 %reduce-scatter.9.cloned.1.call-done = f32[160,1280]{1,0:T(8,128)} async-done(((f32[160,5120]{1,0:T(8,128)}), f32[160,1280]{1,0:T(8,128)}) %reduce-scatter.9.cloned.1.call-update) | async-done | bytes 819216 | tf_op jit(solution)/shard_map/reduce_scatter | solution.py:41
  315.8 2.4 multiply_subtract_fusion
  318.1 133.3 %reduce-scatter.11.cloned.1.call-done = f32[640,1280]{1,0:T(8,128)} async-done(((f32[5120,1280]{1,0:T(8,128)}), f32[640,1280]{1,0:T(8,128)}) %reduce-scatter.11.cloned.1.call-update) | async-done | bytes 3276816 | tf_op jit(solution)/shard_map/reduce_scatter | solution.py:27
  451.4 4.2 multiply_add_fusion
  (19 shorter events, 0.4 us)
Async XLA Ops:
  7.2 45.4 %all-gather.6.cloned.1.call-start = ((), (), s32[]{:S(2)}) async-start(), calls=%async_computation.4 | async-start | bytes 4096000 | tf_op jit(solution)/shard_map/all_gather | solution.py:22
  8.0 3.5 copy-start.5
  8.0 114.1 %all-gather.8.cloned.1.call-start = ((), (), s32[]{:S(2)}) async-start(), calls=%async_computation.5 | async-start | bytes 14745600 | tf_op jit(solution)/shard_map/all_gather | solution.py:31
  11.4 172.2 %reduce-scatter.13.cloned.1.call-start = ((), (), s32[]{:S(2)}) async-start(), calls=%async_computation.10 | async-start | bytes 7372800 | tf_op jit(solution)/shard_map/reduce_scatter | solution.py:34
  142.7 41.0 %copy-start.3 = (f32[160,1280]{1,0:T(8,128)S(1)}, f32[160,1280]{1,0:T(8,128)}, u32[]{:S(2)}) copy-start(f32[160,1280]{1,0:T(8,128)} %param.10) | copy-start | bytes 2457604
  142.7 41.0 %copy-start.4 = (f32[160,1280]{1,0:T(8,128)S(1)}, f32[160,1280]{1,0:T(8,128)}, u32[]{:S(2)}) copy-start(f32[160,1280]{1,0:T(8,128)} %param.11) | copy-start | bytes 2457604
  142.7 82.1 %copy-start.1 = (f32[160,1280]{1,0:T(8,128)S(1)}, f32[160,1280]{1,0:T(8,128)}, u32[]{:S(2)}) copy-start(f32[160,1280]{1,0:T(8,128)} %param.9) | copy-start | bytes 2457604
  142.7 82.1 %all-gather.12.cloned.1.call-start = ((), (), s32[]{:S(2)}) async-start(), calls=%async_computation.8 | async-start | bytes 7372800 | tf_op jit(solution)/shard_map/all_gather | solution.py:23
  143.4 109.1 %all-gather.10.cloned.1.call-start = ((), (), s32[]{:S(2)}) async-start(), calls=%async_computation.6 | async-start | bytes 3686400 | tf_op jit(solution)/shard_map/all_gather | solution.py:38
  186.5 106.3 %reduce-scatter.15.cloned.1.call-start = ((), (), s32[]{:S(2)}) async-start(), calls=%async_computation.11 | async-start | bytes 1638400
  233.1 82.7 %reduce-scatter.9.cloned.1.call-start = ((), (), s32[]{:S(2)}) async-start(), calls=%async_computation.7 | async-start | bytes 4096000 | tf_op jit(solution)/shard_map/reduce_scatter | solution.py:41
  264.9 1.9 copy-start
  264.9 186.5 %reduce-scatter.11.cloned.1.call-start = ((), (), s32[]{:S(2)}) async-start(), calls=%async_computation.9 | async-start | bytes 29491200 | tf_op jit(solution)/shard_map/reduce_scatter | solution.py:27
  292.7 158.7 %copy-start.2 = (f32[640,1280]{1,0:T(8,128)S(1)}, f32[640,1280]{1,0:T(8,128)}, u32[]{:S(2)}) copy-start(f32[640,1280]{1,0:T(8,128)} %param.13) | copy-start | bytes 9830404
Sparse Core Ops, SparseCore 0:
  9.6 42.9 all-gather.5
  54.8 67.2 all-gather.7
  142.8 40.7 reduce-scatter.12
  185.1 39.6 all-gather.11
  226.8 25.6 all-gather.9
  254.7 19.6 reduce-scatter.14
  277.3 38.4 reduce-scatter.8
  318.1 133.2 reduce-scatter.10
where the time goes:
time: 463 us; the launch traced here: 462 us
  waiting for transfers between devices  348 us (75%)
  matrix products  58.9 us (13%)
  other arithmetic  14.3 us (3%)
  between operations  14.2 us (3%)
  blocking collectives  14 us (3%)
  local copies, waits for them, and re-layouts  11.9 us (3%)
    reduce_scatter x1, waiting for transfers between devices, local_step(): lax.psum_scatter(right_part, 'row', scatter_dimension=0, tiled=True)  133 us
    all_gather x1, waiting for transfers between devices, local_step(): lax.all_gather(basis_right.astype(jnp.bfloat16), 'row', axis=0, tiled=True)  69.5 us
    reduce_scatter x1, waiting for transfers between devices, local_step(): lax.psum_scatter(rotated_part, 'row', scatter_dimension=0, tiled=True)  40.2 us
    all_gather x1, waiting for transfers between devices, local_step(): grad_cols = lax.all_gather(grad_in, 'row', axis=0, tiled=True)  38.3 us
    all_gather x1, waiting for transfers between devices, local_step(): grad_rows = lax.all_gather(grad_in, 'col', axis=1, tiled=True)  26.4 us
    dot_general x1, matrix products, local_step(): lax.dot_general(grad_rows, grad_in, contract_rows, precision=highest, pre...  25.9 us
    reduce_scatter x1, waiting for transfers between devices, local_step(): lax.psum_scatter(update_part, 'col', scatter_dimension=1, tiled=True)  20 us
    all_gather x1, waiting for transfers between devices, local_step(): lax.all_gather(direction.astype(jnp.bfloat16), 'row', axis=0, tiled=True)  19.1 us
  transfers between devices with their start and end apart: 8, of which 7 were waited for; matrix products, arithmetic and copies ran while one was open for 13% of the time, Pallas kernels for 0%

commit v1 on v0

v1 whole, which is shorter than its diff:
```python
import jax
import jax.numpy as jnp
from jax import lax
from jax.experimental import pallas as pl
from jax.experimental.pallas import tpu as pltpu
from jax.sharding import PartitionSpec as P

BETA1 = 0.9
BETA2 = 0.9
EPS = 1e-8
LR = 0.1
STEP = 10
BIAS_ONE = 1.0 - BETA1 ** STEP
BIAS_TWO = 1.0 - BETA2 ** STEP
MESH = pl.DeviceIdType.MESH
N_REMOTE = 112
N_LOCAL = 16
F32 = jnp.float32
BF16 = jnp.bfloat16
SIX_PASSES = ((0, 0), (0, 1), (1, 0), (0, 2), (1, 1), (2, 0))


def dot(a, b, dims=((1,), (0,))):
    return lax.dot_general(a, b, (dims, ((), ())), preferred_element_type=F32)


def split_three(a):
    hi = a.astype(BF16)
    rest = a - hi.astype(F32)
    mid = rest.astype(BF16)
    return hi, mid, (rest - mid.astype(F32)).astype(BF16)


def kernel(w_in, g_in, m_in, v_in, l_in, r_in, ql_in, qr_in, w_out, m_out, v_out, l_out, r_out,
           gf, px, rac, qr, grf, gr, qlf, qlr, qlc, wx, mx, vx, h, nb, hp, hx, kb, uc, uf, un,
           lst, lc, lf, ln, lhs3, rhs3, ss, rs, ls):
    rc, cc = g_in.shape
    cr, hc = 2 * rc, cc // 2
    kk = 2 * cr
    nt = 256 if cc % 256 == 0 else cc
    tb = 128 if kk % 128 == 0 else kk
    row, y = lax.axis_index("row"), lax.axis_index("col")
    x, k = row // 2, row % 2
    d = (y - x + 4) % 4

    def ds(start, size, unit=None):
        return pl.ds(start if isinstance(start, int) else pl.multiple_of(start, unit or size), size)

    kcol, ocol = ds(k * hc, hc), ds((1 - k) * hc, hc)
    krow, orow = ds(k * rc, rc), ds((1 - k) * rc, rc)

    counter, pending = [0], []

    def remote(src, dst, dx=0, dk=0, dy=0, index=None, track=True):
        if index is None:
            index = counter[0]
            counter[0] += 1
        assert index < N_REMOTE
        copy = pltpu.make_async_remote_copy(
            src_ref=src, dst_ref=dst, send_sem=ss.at[index], recv_sem=rs.at[index],
            device_id={"row": ((x + dx + 4) % 4) * 2 + (k + dk) % 2, "col": (y + dy + 4) % 4}, device_id_type=MESH)
        if track:
            pending.append(copy)
        return copy

    lcounter = [0]

    def local(src, dst):
        index = lcounter[0]
        lcounter[0] += 1
        assert index < N_LOCAL
        copy = pltpu.make_async_copy(src, dst, ls.at[index])
        copy.start()
        return copy

    class Ring:
        def __init__(self, buf, rows, axis):
            def cp(s0, half, s1, step):
                return remote(buf.at[rows(s0, half)], buf.at[rows(s1, half)], **{axis: step})
            self.ra, self.lb = cp(0, 0, 1, 1), cp(0, 1, 3, -1)
            self.rb, self.la = cp(0, 1, 1, 1), cp(0, 0, 3, -1)
            self.fr, self.fl = cp(1, 0, 2, 1), cp(3, 1, 2, -1)

        def own(self):
            for c in (self.ra, self.lb, self.rb, self.la):
                c.start()

        def fwd(self):
            self.ra.wait_recv()
            self.fr.start()
            self.lb.wait_recv()
            self.fl.start()

        def near(self):
            self.rb.wait_recv()
            self.la.wait_recv()

        def far(self):
            self.fr.wait_recv()
            self.fl.wait_recv()

    def chunked(total, parts, body):
        size = total // parts

        @pl.loop(0, parts)
        def _(i):
            body(ds(i * size, size), i)

    cp_g = local(g_in, gf.at[krow])
    cp_gk = local(g_in.at[:, kcol], grf.at[krow])
    cp_ql = local(ql_in, qlf.at[krow])
    cp_qr = local(qr_in, rac)
    cp_own = [local(a.at[:, kcol], b.at[krow]) for a, b in ((m_in, mx), (v_in, vx), (w_in, wx))]
    cp_l = local(l_in, lst)
    barrier = pltpu.get_barrier_semaphore()
    for dx, dk, dy in ((1, 0, 0), (-1, 0, 0), (2, 0, 0), (0, 1, 0), (0, 0, 1), (0, 0, -1)):
        pl.semaphore_signal(barrier, inc=1, device_id={"row": ((x + dx + 4) % 4) * 2 + (k + dk) % 2, "col": (y + dy + 4) % 4},
                            device_id_type=MESH)
    pl.semaphore_wait(barrier, 6)

    d_gk = remote(g_in.at[:, ocol], grf.at[krow], dk=1)
    d_ql = remote(ql_in, qlf.at[krow], dk=1)
    d_g0 = remote(g_in, gf.at[krow], dk=1)
    d_own = [remote(a.at[:, ocol], b.at[krow], dk=1) for a, b in ((m_in, mx), (v_in, vx), (w_in, wx))]
    d_gk.start()
    d_ql.start()

    def grow(s, half):
        return ds((s * 2 + k) * rc + half * (rc // 2), rc // 2)

    def slot_rows(n):
        return lambda s, half: ds(s * n + half * (n // 2), n // 2)

    x1 = Ring(gf, grow, "dx")
    x2 = Ring(qr, slot_rows(hc), "dx")
    x3 = Ring(h, slot_rows(cr), "dx")
    x4 = Ring(nb, slot_rows(cr), "dx")
    y1 = Ring(gr, slot_rows(cr), "dy")
    y2 = Ring(qlr, slot_rows(cr), "dy")

    cp_g.wait()
    x1.own()
    cp_gk.wait()
    d_gk.wait_recv()
    chunked(cr, 4, lambda r, i: gr.__setitem__((r, slice(None)), grf[r, :].astype(BF16)))
    y1.own()
    cp_ql.wait()
    d_ql.wait_recv()
    qlr[ds(0, cr), :] = qlf[...].astype(BF16)
    y2.own()
    d_g0.start()
    for c in d_own:
        c.start()
    cp_qr.wait()
    chunked(hc, 8, lambda r, i: qr.__setitem__((r, slice(None)), rac[r, :].astype(BF16)))
    cp_r = local(r_in, rac)

    x1.fwd()
    x2.own()
    y1.fwd()
    y2.fwd()
    x1.near()

    def whole(s):
        return ds((s * 2 + k) * rc, rc)

    d_g = {s: remote(gf.at[whole(s)], gf.at[whole(s)], dk=1) for s in (1, 3, 2)}
    d_g[1].start()
    d_g[3].start()

    def prow(s, c):
        return ds((s * 2 + c) * rc, rc)

    p_src, p_fwd, q_src, q_fwd = {}, {}, {}, {}
    for s in (0, 1, 3, 2):
        pi, qi = counter[0], counter[0] + 1
        counter[0] += 2
        p_src[s] = remote(gf.at[prow(s, 0), kcol], px.at[prow(s, 0)], dy=1, index=pi, track=False)
        p_fwd[s] = remote(px.at[prow(s, 0)], px.at[prow(s, 0)], dy=1, index=pi, track=False)
        q_src[s] = remote(gf.at[prow(s, 1), kcol], px.at[prow(s, 1)], dy=-1, index=qi, track=False)
        q_fwd[s] = remote(px.at[prow(s, 1)], px.at[prow(s, 1)], dy=-1, index=qi, track=False)

    def panel_source(s):
        @pl.when(d == 0)
        def _():
            p_src[s].start()
            q_src[s].start()

    def panel_relay(s):
        @pl.when(d == 3)
        def _():
            q_fwd[s].wait_recv()
            q_fwd[s].start()

        @pl.when(d != 0)
        def _():
            p_fwd[s].wait_recv()

        @pl.when((d == 1) | (d == 2))
        def _():
            p_fwd[s].start()
            q_fwd[s].wait_recv()

        @pl.when(d == 2)
        def _():
            q_fwd[s].start()

    d_g0.wait_recv()
    panel_source(0)
    y1.near()
    y2.near()
    y1.far()
    y2.far()
    d_g[1].wait_recv()
    panel_source(1)
    d_g[3].wait_recv()
    panel_source(3)

    qlc[ds(0, cr), :] = qlr[ds(d * cr, cr), :]
    a2a = []
    for s in (1, 3, 2):
        t = (y - x - s + 8) % 4
        a2a.append((s, remote(qlr.at[ds(t * cr + k * rc, rc, rc)], qlc.at[whole(s)], dx=s)))
        a2a[-1][1].start()

    def h_part(s):
        t = (d + s) % 4

        def body(cols, i):
            part = dot(gr[ds(t * cr, cr), :], qr[ds(s * hc, hc), cols])
            if s == 0:
                hp[:, cols] = part
            else:
                hp[:, cols] += part

        chunked(cc, cc // nt, lambda cols, i: body(cols, i))

    h_part(0)
    x1.far()
    d_g[2].start()
    panel_relay(0)
    panel_relay(1)
    d_c = [remote(qlc.at[whole(s)], qlc.at[whole(s)], dk=1) for s, _ in a2a]
    for (s, c), e in zip(a2a, d_c):
        c.wait_recv()
        e.start()
    d_g[2].wait_recv()
    panel_source(2)

    def r_piece(p):
        base = p * kk

        @pl.when(d == 0)
        def _():
            chunked(kk, 4, lambda r, i: px.__setitem__(
                (ds(base + i * (kk // 4), kk // 4, 8), slice(None)), gf[ds(base + i * (kk // 4), kk // 4, 8), kcol]))

        def split_right(r, i):
            for q, piece in enumerate(split_three(gf[ds(base + i * (kk // 8), kk // 8, 8), :])):
                rhs3[ds(q * kk + i * (kk // 8), kk // 8, 8), :] = piece

        chunked(kk, 8, split_right)

        def split_left(cols, i):
            for q, piece in enumerate(split_three(px[ds(base + i * tb, tb, 8), :].T)):
                lhs3[ds(q * hc, hc), cols] = piece

        chunked(kk, kk // tb, split_left)

        def product(rows2, cols):
            acc = sum(dot(lhs3[ds(a * hc + rows2 * (hc // 2), hc // 2, 8), :], rhs3[ds(b * kk, kk), cols]) for a, b in SIX_PASSES)
            at = (ds(rows2 * (hc // 2), hc // 2), cols)
            if p == 0:
                rac[at] = BETA2 * rac[at] + (1.0 - BETA2) * acc
            else:
                rac[at] += (1.0 - BETA2) * acc

        @pl.loop(0, 2)
        def _(m):
            chunked(cc, cc // nt, lambda cols, i: product(m, cols))

    cp_r.wait()
    r_piece(0)
    x2.fwd()
    panel_relay(3)
    panel_relay(2)
    r_piece(1)
    out_r = local(rac, r_out)

    class Sum:
        def __init__(self, buf, far, near, n, compute):
            self.buf, self.far_, self.near_, self.n, self.compute = buf, far, near, n, compute
            hn = n // 2
            self.rows = lambda e, half: ds(e * n + half * hn, hn)
            rows = self.rows
            self.fa = remote(buf.at[rows(2, 0)], far.at[ds(0, hn)], dy=1)
            self.fb = remote(buf.at[rows(2, 1)], far.at[ds(hn, hn)], dy=-1)
            self.r1b = remote(buf.at[rows(1, 1)], near.at[ds(hn, hn)], dy=1)
            self.l1a = remote(buf.at[rows(3, 0)], near.at[ds(n, hn)], dy=-1)
            self.r1a = remote(buf.at[rows(1, 0)], near.at[ds(0, hn)], dy=1)
            self.l1b = remote(buf.at[rows(3, 1)], near.at[ds(n + hn, hn)], dy=-1)

        def begin(self):
            self.compute(2)
            self.fa.start()
            self.fb.start()
            self.compute(1)
            self.r1b.start()
            self.compute(3)
            self.l1a.start()
            self.compute(0)

        def middle(self):
            hn, buf, far, rows = self.n // 2, self.buf, self.far_, self.rows
            self.fa.wait_recv()
            buf[rows(1, 0), :] += far[ds(0, hn), :]
            self.r1a.start()
            self.fb.wait_recv()
            buf[rows(3, 1), :] += far[ds(hn, hn), :]
            self.l1b.start()

        def finish(self):
            for c in (self.r1b, self.l1a, self.r1a, self.l1b):
                c.wait_recv()

        def total(self, start, size):
            n = self.n
            return self.buf[ds(start, size, 8), :] + (self.near_[ds(start, size, 8), :] + self.near_[ds(n + start, size, 8), :])

    for q, piece in enumerate(split_three(gf[krow, :])):
        rhs3[ds(3 * cr + q * rc, rc), :] = piece

    def l_chunk(e):
        s = (x - y - e + 8) % 4

        def split_block(r, i):
            for q, piece in enumerate(split_three(gf[ds(s * cr + i * (cr // 4), cr // 4, 8), :])):
                rhs3[ds(q * cr + i * (cr // 4), cr // 4, 8), :] = piece

        chunked(cr, 4, split_block)
        lc[ds(e * rc, rc), :] = sum(
            dot(rhs3[ds(3 * cr + a * rc, rc), :], rhs3[ds(b * cr, cr), :], ((1,), (1,))) for a, b in SIX_PASSES)

    l_sum = Sum(lc, lf, ln, rc, l_chunk)
    l_sum.begin()
    l_sum.middle()

    x2.near()
    h_part(1)
    h_part(3)
    x2.far()
    h_part(2)
    d_h = remote(hp.at[:, ocol], hx, dk=1)
    d_h.start()
    d_h.wait_recv()
    chunked(cr, 4, lambda r, i: h.__setitem__((r, slice(None)), (hp[r, kcol] + hx[r, :]).astype(BF16)))
    x3.own()
    l_sum.finish()
    cp_l.wait()
    lst[...] = BETA2 * lst[...] + (1.0 - BETA2) * l_sum.total(0, rc)
    out_l = local(lst, l_out)
    for c in cp_own:
        c.wait()
    for c in d_own:
        c.wait_recv()
    for c in d_c:
        c.wait_recv()
    x3.fwd()
    x3.near()
    x3.far()

    hx[...] = dot(qlc[...], h[...], ((0,), (0,)))

    def moments(r, i):
        rotated = hx[r, :]
        new_first = BETA1 * mx[r, :] + (1.0 - BETA1) * rotated
        new_second = BETA2 * vx[r, :] + (1.0 - BETA2) * rotated * rotated
        mx[r, :] = new_first
        vx[r, :] = new_second
        direction = (new_first / BIAS_ONE) / (jnp.sqrt(new_second / BIAS_TWO) + EPS)
        nb[r, :] = direction.astype(BF16)

    chunked(cr, 10 if cr % 160 == 0 else 1, moments)
    x4.own()
    outs = []
    for buf, out in ((mx, m_out), (vx, v_out)):
        outs.append(remote(buf.at[orow], out.at[:, kcol], dk=1))
        outs[-1].start()
    out_own = [local(buf.at[krow], out.at[:, kcol]) for buf, out in ((mx, m_out), (vx, v_out))]
    x4.fwd()
    x4.near()
    x4.far()

    kval = sum(dot(qlr[ds(((d + s) % 4) * cr, cr), :], nb[ds(s * cr, cr), :]) for s in range(4))
    kb[ds(k * cr, cr), :] = kval.astype(BF16)
    d_k = remote(kb.at[ds(k * cr, cr)], kb.at[ds(k * cr, cr)], dk=1)
    d_k.start()
    d_k.wait_recv()

    def u_chunk(e):
        s = (x - y - e + 8) % 4
        rows = ds(s * hc, hc)
        uc[ds(e * cr, cr), :] = (dot(kb[ds(0, cr), :], qr[rows, ds(0, hc)], ((1,), (1,)))
                                 + dot(kb[ds(cr, cr), :], qr[rows, ds(hc, hc)], ((1,), (1,))))

    u_sum = Sum(uc, uf, un, cr, u_chunk)
    u_sum.begin()
    u_sum.middle()
    u_sum.finish()

    def final(r, i):
        wx[r, :] = wx[r, :] - LR * u_sum.total(i * (cr // 4), cr // 4)

    chunked(cr, 4, final)
    outs.append(remote(wx.at[orow], w_out.at[:, kcol], dk=1))
    outs[-1].start()
    out_own.append(local(wx.at[krow], w_out.at[:, kcol]))
    for c in outs:
        c.wait_recv()
    for c in out_own + [out_l, out_r]:
        c.wait()
    for c in pending:
        c.wait_send()
    for s in (0, 1, 3, 2):
        @pl.when(d != 3)
        def _():
            p_fwd[s].wait_send()

        @pl.when(d != 1)
        def _():
            q_fwd[s].wait_send()


def solution(mesh):
    tile_spec = P(("layer", "row"), "col")

    def step(weight, grad_in, mom_first, mom_second, stat_left, stat_right, basis_left, basis_right):
        rc, cc = grad_in.shape
        cr, hc, q = 2 * rc, cc // 2, basis_left.shape[1]
        scratch = [
            ((4 * cr, cc), F32), ((4 * cr, hc), F32), ((hc, cc), F32), ((4 * hc, cc), BF16),
            ((cr, hc), F32), ((4 * cr, hc), BF16),
            ((cr, q), F32), ((4 * cr, q), BF16), ((4 * cr, q), BF16),
            ((cr, hc), F32), ((cr, hc), F32), ((cr, hc), F32),
            ((4 * cr, hc), BF16), ((4 * cr, hc), BF16), ((cr, cc), F32), ((cr, hc), F32),
            ((2 * cr, hc), BF16), ((4 * cr, hc), F32), ((cr, hc), F32), ((2 * cr, hc), F32),
            ((rc, q), F32), ((4 * rc, q), F32), ((rc, q), F32), ((2 * rc, q), F32),
            ((3 * hc, 2 * cr), BF16), ((6 * cr, cc), BF16),
        ]
        args = (weight, grad_in, mom_first, mom_second, stat_left, stat_right, basis_left, basis_right)
        any_spec = pl.BlockSpec(memory_space=pl.ANY)
        return pl.pallas_call(
            kernel,
            out_shape=tuple(jax.ShapeDtypeStruct(a.shape, F32)
                            for a in (weight, mom_first, mom_second, stat_left, stat_right)),
            in_specs=[any_spec] * 8,
            out_specs=(any_spec,) * 5,
            scratch_shapes=[pltpu.VMEM(s, t) for s, t in scratch]
            + [pltpu.SemaphoreType.DMA((N_REMOTE,)), pltpu.SemaphoreType.DMA((N_REMOTE,)), pltpu.SemaphoreType.DMA((N_LOCAL,))],
            compiler_params=pltpu.CompilerParams(collective_id=0, has_side_effects=True, vmem_limit_bytes=67_000_000),
        )(*args)

    return jax.shard_map(step, mesh=mesh, in_specs=(tile_spec,) * 8, out_specs=(tile_spec,) * 5, check_vma=False)
```

time: 463 us -> 235 us (0.51)
  waiting for transfers between devices: 348 us -> 0 us
  Pallas kernels: 0 us -> 226 us
  matrix products: 58.9 us -> 0 us
  other arithmetic: 14.3 us -> 0 us
  blocking collectives: 14 us -> 0 us
  between operations: 14.2 us -> 0.66 us
    pallas_call x0 -> x1, Pallas kernels: none -> 226 us  [step(): pl.pallas_call(kernel, out_shape=tuple((jax.ShapeDtypeStruct(a.shape, F32...]
    reduce_scatter x3 -> x0, waiting for transfers between devices: 194 us -> none  [the longest x1 133 us: local_step(): lax.psum_scatter(right_part, 'row', scatter_dimension=0, tiled=True)]
    all_gather x4 -> x0, waiting for transfers between devices: 153 us -> none  [the longest x1 69.5 us: local_step(): lax.all_gather(basis_right.astype(jnp.bfloat16), 'row', axis=0, tiled=True)]
    dot_general x3 -> x0, matrix products: 50.7 us -> none  [the longest x1 25.9 us: local_step(): lax.dot_general(grad_rows, grad_in, contract_rows, precision=highest, pre...]
    all_gather x1 -> x0, blocking collectives: 14 us -> none  [local_step(): lax.all_gather(basis_left.astype(jnp.bfloat16), 'col', axis=1, tiled=True)]
    unnamed x1 -> x0, matrix products: 8.23 us -> none
    convert_element_type x2 -> x0, other arithmetic: 6.06 us -> none  [the longest x1 3.29 us: local_step(): basis_right.astype(jnp.bfloat16)]
    add x2 -> x0, other arithmetic: 5.83 us -> none  [the longest x1 4.16 us: local_step(): new_right = BETA2 * stat_right + (1.0 - BETA2) * right_sum]
  transfers between devices with their start and end apart: 8 -> 0, of which waited for: 7 -> 0; matrix products, arithmetic and copies ran while one was open for 13% -> 0% of each run, Pallas kernels for 0% -> 0%
where the time goes in v1:
time: 235 us
  Pallas kernels  226 us (96%)
  local copies, waits for them, and re-layouts  8.82 us (4%)
    pallas_call x1, Pallas kernels, step(): pl.pallas_call(kernel, out_shape=tuple((jax.ShapeDtypeStruct(a.shape, F32...  226 us
    unnamed x9, local copies, waits for them, and re-layouts  8.82 us

profile of v1, /device:TPU:97, one launch (start us, length us, event | category | flops | bytes accessed | tf_op | source)
XLA Modules:
  0.0 235.3 jit_solution(3589337450340047950)
XLA Ops:
  0.6 225.8 %shard_map.119 = (f32[160,1280]{1,0:T(8,128)}, f32[160,1280]{1,0:T(8,128)}, f32[160,1280]{1,0:T(8,128)}, f32[160,320]{1,0:T(8,128)}, f32[640,1280]{1,0:T(8,128)}) custom-call(f32[160,1280]{1,0:T(8,128)} %w_in.1, f32[160,1280]{1,0:T(8,128)} %g_in.1, f32[160,1280]{1,0:T(8,128)} %m_in.1, f32[160,1280]{1,0:T(8,128)} %v_in.1, f32[160,320]{1,0:T(8,128)} %l_in.1, ...), custom_call_target="tpu_custom_call" | custom-call | tf_op jit(solution)/shard_map/pallas_call | solution.py:452
  226.5 0.0 copy-start.1
  226.5 0.0 copy-start
  226.5 2.2 copy.18
  228.7 2.1 copy.19
  230.8 2.1 copy.20
  232.9 0.0 copy-done.1
  232.9 0.7 copy.21
  233.6 0.0 copy-done
  233.6 1.7 copy.22
Async XLA Ops:
  226.5 6.4 %copy-start.1 = (f32[160,320]{1,0:T(8,128)S(1)}, f32[160,320]{1,0:T(8,128)}, u32[]{:S(2)}) copy-start(f32[160,320]{1,0:T(8,128)} %get-tuple-element.13) | copy-start | bytes 614404
  226.5 7.1 %copy-start = (f32[640,1280]{1,0:T(8,128)S(1)}, f32[640,1280]{1,0:T(8,128)}, u32[]{:S(2)}) copy-start(f32[640,1280]{1,0:T(8,128)} %get-tuple-element.14) | copy-start | bytes 9830404

commit v2 on v1

--- a/solution.py
+++ b/solution.py
@@ -33,7 +33,7 @@
 
 def kernel(w_in, g_in, m_in, v_in, l_in, r_in, ql_in, qr_in, w_out, m_out, v_out, l_out, r_out,
            gf, px, rac, qr, grf, gr, qlf, qlr, qlc, wx, mx, vx, h, nb, hp, hx, kb, uc, uf, un,
-           lst, lc, lf, ln, lhs3, rhs3, ss, rs, ls):
+           lst, lc, lf, ln, lhs3, rhs3, la, ss, rs, ls):
     rc, cc = g_in.shape
     cr, hc = 2 * rc, cc // 2
     kk = 2 * cr
@@ -119,9 +119,10 @@
     pl.semaphore_wait(barrier, 6)
 
     d_gk = remote(g_in.at[:, ocol], grf.at[krow], dk=1)
+    d_g0 = remote(g_in, gf.at[krow], dk=1)
     d_ql = remote(ql_in, qlf.at[krow], dk=1)
-    d_g0 = remote(g_in, gf.at[krow], dk=1)
     d_own = [remote(a.at[:, ocol], b.at[krow], dk=1) for a, b in ((m_in, mx), (v_in, vx), (w_in, wx))]
+    d_g0.start()
     d_gk.start()
     d_ql.start()
 
@@ -130,6 +131,9 @@
 
     def slot_rows(n):
         return lambda s, half: ds(s * n + half * (n // 2), n // 2)
+
+    def whole(s):
+        return ds((s * 2 + k) * rc, rc)
 
     x1 = Ring(gf, grow, "dx")
     x2 = Ring(qr, slot_rows(hc), "dx")
@@ -137,36 +141,7 @@
     x4 = Ring(nb, slot_rows(cr), "dx")
     y1 = Ring(gr, slot_rows(cr), "dy")
     y2 = Ring(qlr, slot_rows(cr), "dy")
-
-    cp_g.wait()
-    x1.own()
-    cp_gk.wait()
-    d_gk.wait_recv()
-    chunked(cr, 4, lambda r, i: gr.__setitem__((r, slice(None)), grf[r, :].astype(BF16)))
-    y1.own()
-    cp_ql.wait()
-    d_ql.wait_recv()
-    qlr[ds(0, cr), :] = qlf[...].astype(BF16)
-    y2.own()
-    d_g0.start()
-    for c in d_own:
-        c.start()
-    cp_qr.wait()
-    chunked(hc, 8, lambda r, i: qr.__setitem__((r, slice(None)), rac[r, :].astype(BF16)))
-    cp_r = local(r_in, rac)
-
-    x1.fwd()
-    x2.own()
-    y1.fwd()
-    y2.fwd()
-    x1.near()
-
-    def whole(s):
-        return ds((s * 2 + k) * rc, rc)
-
     d_g = {s: remote(gf.at[whole(s)], gf.at[whole(s)], dk=1) for s in (1, 3, 2)}
-    d_g[1].start()
-    d_g[3].start()
 
     def prow(s, c):
         return ds((s * 2 + c) * rc, rc)
@@ -186,68 +161,55 @@
             p_src[s].start()
             q_src[s].start()
 
-    def panel_relay(s):
+    def panel_first(s):
+        @pl.when(d == 1)
+        def _():
+            p_fwd[s].wait_recv()
+            p_fwd[s].start()
+
         @pl.when(d == 3)
         def _():
             q_fwd[s].wait_recv()
             q_fwd[s].start()
 
-        @pl.when(d != 0)
+    def panel_second(s):
+        @pl.when(d == 2)
         def _():
             p_fwd[s].wait_recv()
-
-        @pl.when((d == 1) | (d == 2))
-        def _():
             p_fwd[s].start()
             q_fwd[s].wait_recv()
-
-        @pl.when(d == 2)
-        def _():
             q_fwd[s].start()
 
-    d_g0.wait_recv()
-    panel_source(0)
-    y1.near()
-    y2.near()
-    y1.far()
-    y2.far()
-    d_g[1].wait_recv()
-    panel_source(1)
-    d_g[3].wait_recv()
-    panel_source(3)
-
-    qlc[ds(0, cr), :] = qlr[ds(d * cr, cr), :]
-    a2a = []
-    for s in (1, 3, 2):
-        t = (y - x - s + 8) % 4
-        a2a.append((s, remote(qlr.at[ds(t * cr + k * rc, rc, rc)], qlc.at[whole(s)], dx=s)))
-        a2a[-1][1].start()
-
-    def h_part(s):
+    def panel_third(s):
+        @pl.when(d == 3)
+        def _():
+            p_fwd[s].wait_recv()
+
+        @pl.when(d == 1)
+        def _():
+            q_fwd[s].wait_recv()
+
+    def h_part(s, cols):
         t = (d + s) % 4
-
-        def body(cols, i):
-            part = dot(gr[ds(t * cr, cr), :], qr[ds(s * hc, hc), cols])
-            if s == 0:
-                hp[:, cols] = part
-            else:
-                hp[:, cols] += part
-
-        chunked(cc, cc // nt, lambda cols, i: body(cols, i))
-
-    h_part(0)
-    x1.far()
-    d_g[2].start()
-    panel_relay(0)
-    panel_relay(1)
-    d_c = [remote(qlc.at[whole(s)], qlc.at[whole(s)], dk=1) for s, _ in a2a]
-    for (s, c), e in zip(a2a, d_c):
-        c.wait_recv()
-        e.start()
-    d_g[2].wait_recv()
-    panel_source(2)
-
-    def r_piece(p):
+        part = dot(gr[ds(t * cr, cr), :], qr[ds(s * hc, hc), cols])
+        if s == 0:
+            hp[:, cols] = part
+        else:
+            hp[:, cols] += part
+
+    def split_right(p):
+        base = p * kk
+
+        def body(r, i):
+            for q, piece in enumerate(split_three(gf[ds(base + i * (kk // 8), kk // 8, 8), :])):
+                rhs3[ds(q * kk + i * (kk // 8), kk // 8, 8), :] = piece
+
+        chunked(kk, 8, body)
+        if p == 0:
+            for q in range(3):
+                la[ds(q * rc, rc), :] = rhs3[ds(q * kk + k * rc, rc, rc), :]
+
+    def split_left(p):
         base = p * kk
 
         @pl.when(d == 0)
@@ -255,37 +217,30 @@
             chunked(kk, 4, lambda r, i: px.__setitem__(
                 (ds(base + i * (kk // 4), kk // 4, 8), slice(None)), gf[ds(base + i * (kk // 4), kk // 4, 8), kcol]))
 
-        def split_right(r, i):
-            for q, piece in enumerate(split_three(gf[ds(base + i * (kk // 8), kk // 8, 8), :])):
-                rhs3[ds(q * kk + i * (kk // 8), kk // 8, 8), :] = piece
-
-        chunked(kk, 8, split_right)
-
-        def split_left(cols, i):
+        def body(cols, i):
             for q, piece in enumerate(split_three(px[ds(base + i * tb, tb, 8), :].T)):
                 lhs3[ds(q * hc, hc), cols] = piece
 
-        chunked(kk, kk // tb, split_left)
-
-        def product(rows2, cols):
-            acc = sum(dot(lhs3[ds(a * hc + rows2 * (hc // 2), hc // 2, 8), :], rhs3[ds(b * kk, kk), cols]) for a, b in SIX_PASSES)
-            at = (ds(rows2 * (hc // 2), hc // 2), cols)
+        chunked(kk, kk // tb, body)
+
+    def product(p, m):
+        def body(cols, i):
+            acc = sum(dot(lhs3[ds(a * hc + m * (hc // 2), hc // 2), :], rhs3[ds(b * kk, kk), cols]) for a, b in SIX_PASSES)
+            at = (ds(m * (hc // 2), hc // 2), cols)
             if p == 0:
                 rac[at] = BETA2 * rac[at] + (1.0 - BETA2) * acc
             else:
                 rac[at] += (1.0 - BETA2) * acc
 
-        @pl.loop(0, 2)
-        def _(m):
-            chunked(cc, cc // nt, lambda cols, i: product(m, cols))
-
-    cp_r.wait()
-    r_piece(0)
-    x2.fwd()
-    panel_relay(3)
-    panel_relay(2)
-    r_piece(1)
-    out_r = local(rac, r_out)
+        chunked(cc, cc // nt, body)
+
+    def l_slot(s):
+        e = (x - y - s + 8) % 4
+        at = [ds(q * kk + (s % 2) * cr, cr) for q in range(3)]
+        high = dot(la[...], rhs3[at[0], :], ((1,), (1,)))
+        middle = dot(la[ds(0, 2 * rc), :], rhs3[at[1], :], ((1,), (1,)))
+        low = dot(la[ds(0, rc), :], rhs3[at[2], :], ((1,), (1,)))
+        lc[ds(e * rc, rc), :] = high[:rc] + (high[rc:2 * rc] + middle[:rc]) + (high[2 * rc:] + middle[rc:] + low)
 
     class Sum:
         def __init__(self, buf, far, near, n, compute):
@@ -327,45 +282,98 @@
             n = self.n
             return self.buf[ds(start, size, 8), :] + (self.near_[ds(start, size, 8), :] + self.near_[ds(n + start, size, 8), :])
 
-    for q, piece in enumerate(split_three(gf[krow, :])):
-        rhs3[ds(3 * cr + q * rc, rc), :] = piece
-
-    def l_chunk(e):
-        s = (x - y - e + 8) % 4
-
-        def split_block(r, i):
-            for q, piece in enumerate(split_three(gf[ds(s * cr + i * (cr // 4), cr // 4, 8), :])):
-                rhs3[ds(q * cr + i * (cr // 4), cr // 4, 8), :] = piece
-
-        chunked(cr, 4, split_block)
-        lc[ds(e * rc, rc), :] = sum(
-            dot(rhs3[ds(3 * cr + a * rc, rc), :], rhs3[ds(b * cr, cr), :], ((1,), (1,))) for a, b in SIX_PASSES)
-
-    l_sum = Sum(lc, lf, ln, rc, l_chunk)
-    l_sum.begin()
-    l_sum.middle()
-
+    cp_g.wait()
+    x1.own()
+    d_g0.wait_recv()
+    panel_source(0)
+    cp_gk.wait()
+    d_gk.wait_recv()
+    chunked(cr, 4, lambda r, i: gr.__setitem__((r, slice(None)), grf[r, :].astype(BF16)))
+    y1.own()
+    cp_ql.wait()
+    d_ql.wait_recv()
+    qlr[ds(0, cr), :] = qlf[...].astype(BF16)
+    for c in d_own:
+        c.start()
+    cp_qr.wait()
+    chunked(hc, 8, lambda r, i: qr.__setitem__((r, slice(None)), rac[r, :].astype(BF16)))
+    cp_r = local(r_in, rac)
+    x1.fwd()
+    x2.own()
+    panel_first(0)
+    y1.fwd()
+    x1.near()
+    d_g[1].start()
+    d_g[3].start()
+    d_g[1].wait_recv()
+    panel_source(1)
+    d_g[3].wait_recv()
+    panel_source(3)
+    y1.near()
+    y1.far()
+    h_part(0, ocol)
+    h_part(0, kcol)
+    x1.far()
+    d_g[2].start()
+    d_g[2].wait_recv()
+    panel_source(2)
+    y2.own()
+    split_right(0)
+    panel_first(1)
+    panel_second(0)
+    panel_first(3)
+    panel_second(1)
+    panel_third(0)
+    x2.fwd()
+    panel_first(2)
+    panel_second(3)
+    panel_third(1)
+    y2.fwd()
+    cp_r.wait()
+    split_left(0)
+    product(0, 0)
+    product(0, 1)
+    l_slot(0)
+    l_slot(1)
     x2.near()
-    h_part(1)
-    h_part(3)
+    for s in (1, 3):
+        h_part(s, ocol)
+        h_part(s, kcol)
+    y2.near()
+    y2.far()
+    qlc[ds(0, cr), :] = qlr[ds(d * cr, cr), :]
+    a2a = []
+    for s in (1, 3, 2):
+        t = (y - x - s + 8) % 4
+        a2a.append(remote(qlr.at[ds(t * cr + k * rc, rc, rc)], qlc.at[whole(s)], dx=s))
+        a2a[-1].start()
+    d_c = [remote(qlc.at[whole(s)], qlc.at[whole(s)], dk=1) for s in (1, 3, 2)]
+    panel_second(2)
+    panel_third(3)
+    split_right(1)
     x2.far()
-    h_part(2)
     d_h = remote(hp.at[:, ocol], hx, dk=1)
+    h_part(2, ocol)
     d_h.start()
+    h_part(2, kcol)
     d_h.wait_recv()
     chunked(cr, 4, lambda r, i: h.__setitem__((r, slice(None)), (hp[r, kcol] + hx[r, :]).astype(BF16)))
     x3.own()
-    l_sum.finish()
-    cp_l.wait()
-    lst[...] = BETA2 * lst[...] + (1.0 - BETA2) * l_sum.total(0, rc)
-    out_l = local(lst, l_out)
+    panel_third(2)
+    split_left(1)
+    product(1, 0)
+    x3.fwd()
+    product(1, 1)
+    out_r = local(rac, r_out)
+    for c, e in zip(a2a, d_c):
+        c.wait_recv()
+        e.start()
     for c in cp_own:
         c.wait()
     for c in d_own:
         c.wait_recv()
     for c in d_c:
         c.wait_recv()
-    x3.fwd()
     x3.near()
     x3.far()
 
@@ -387,7 +395,12 @@
         outs.append(remote(buf.at[orow], out.at[:, kcol], dk=1))
         outs[-1].start()
     out_own = [local(buf.at[krow], out.at[:, kcol]) for buf, out in ((mx, m_out), (vx, v_out))]
+    l_slot(2)
+    l_slot(3)
+    l_sum = Sum(lc, lf, ln, rc, lambda e: None)
+    l_sum.begin()
     x4.fwd()
+    l_sum.middle()
     x4.near()
     x4.far()
 
@@ -405,6 +418,10 @@
 
     u_sum = Sum(uc, uf, un, cr, u_chunk)
     u_sum.begin()
+    l_sum.finish()
+    cp_l.wait()
+    lst[...] = BETA2 * lst[...] + (1.0 - BETA2) * l_sum.total(0, rc)
+    out_l = local(lst, l_out)
     u_sum.middle()
     u_sum.finish()
 
@@ -431,6 +448,27 @@
             q_fwd[s].wait_send()
 
 
+def copy_kernel(*refs):
+    n = (len(refs) - 2) // 3
+    ins, outs, bufs, (si, so) = refs[:n], refs[n:2 * n], refs[2 * n:3 * n], refs[3 * n:]
+    parts, reads, writes = [], [], []
+    for a, b, o in zip(ins, bufs, outs):
+        rows = a.shape[0]
+        step = rows // 4 if rows % 32 == 0 and rows >= 512 else rows
+        for r in range(0, rows, step):
+            at = pl.ds(r, step)
+            i = len(reads)
+            reads.append(pltpu.make_async_copy(a.at[at], b.at[at], si.at[i]))
+            writes.append(pltpu.make_async_copy(b.at[at], o.at[at], so.at[i]))
+    for c in reads:
+        c.start()
+    for c, e in zip(reads, writes):
+        c.wait()
+        e.start()
+    for e in writes:
+        e.wait()
+
+
 def solution(mesh):
     tile_spec = P(("layer", "row"), "col")
 
@@ -445,11 +483,11 @@
             ((4 * cr, hc), BF16), ((4 * cr, hc), BF16), ((cr, cc), F32), ((cr, hc), F32),
             ((2 * cr, hc), BF16), ((4 * cr, hc), F32), ((cr, hc), F32), ((2 * cr, hc), F32),
             ((rc, q), F32), ((4 * rc, q), F32), ((rc, q), F32), ((2 * rc, q), F32),
-            ((3 * hc, 2 * cr), BF16), ((6 * cr, cc), BF16),
+            ((3 * hc, 2 * cr), BF16), ((6 * cr, cc), BF16), ((3 * rc, cc), BF16),
         ]
         args = (weight, grad_in, mom_first, mom_second, stat_left, stat_right, basis_left, basis_right)
         any_spec = pl.BlockSpec(memory_space=pl.ANY)
-        return pl.pallas_call(
+        sums = pl.pallas_call(
             kernel,
             out_shape=tuple(jax.ShapeDtypeStruct(a.shape, F32)
                             for a in (weight, mom_first, mom_second, stat_left, stat_right)),
@@ -459,5 +497,12 @@
             + [pltpu.SemaphoreType.DMA((N_REMOTE,)), pltpu.SemaphoreType.DMA((N_REMOTE,)), pltpu.SemaphoreType.DMA((N_LOCAL,))],
             compiler_params=pltpu.CompilerParams(collective_id=0, has_side_effects=True, vmem_limit_bytes=67_000_000),
         )(*args)
+        return pl.pallas_call(
+            copy_kernel,
+            out_shape=tuple(jax.ShapeDtypeStruct(a.shape, F32) for a in sums),
+            in_specs=[any_spec] * 5,
+            out_specs=(any_spec,) * 5,
+            scratch_shapes=[pltpu.VMEM(a.shape, F32) for a in sums] + [pltpu.SemaphoreType.DMA((20,))] * 2,
+        )(*sums)
 
     return jax.shard_map(step, mesh=mesh, in_specs=(tile_spec,) * 8, out_specs=(tile_spec,) * 5, check_vma=False)

time: 235 us -> 168 us (0.71)
  Pallas kernels: 226 us -> 167 us
  local copies, waits for them, and re-layouts: 8.82 us -> 0 us
    pallas_call x1, Pallas kernels: 226 us -> 162 us  [step(): pl.pallas_call(kernel, out_shape=tuple((jax.ShapeDtypeStruct(a.shape, F32...]
    unnamed x9 -> x0, local copies, waits for them, and re-layouts: 8.82 us -> none
    pallas_call x0 -> x1, Pallas kernels: none -> 5.51 us  [step(): pl.pallas_call(copy_kernel, out_shape=tuple((jax.ShapeDtypeStruct(a.shape...]
where the time goes in v2:
time: 168 us
  Pallas kernels  167 us (99%)
    pallas_call x1, Pallas kernels, step(): pl.pallas_call(kernel, out_shape=tuple((jax.ShapeDtypeStruct(a.shape, F32...  162 us
    pallas_call x1, Pallas kernels, step(): pl.pallas_call(copy_kernel, out_shape=tuple((jax.ShapeDtypeStruct(a.shape...  5.51 us

profile of v2, /device:TPU:97, one launch (start us, length us, event | category | flops | bytes accessed | tf_op | source)
XLA Modules:
  0.0 168.1 jit_solution(12681631022760428084)
XLA Ops:
  0.6 161.8 %shard_map.119 = (f32[160,1280]{1,0:T(8,128)}, f32[160,1280]{1,0:T(8,128)}, f32[160,1280]{1,0:T(8,128)}, f32[160,320]{1,0:T(8,128)}, f32[640,1280]{1,0:T(8,128)}) custom-call(f32[160,1280]{1,0:T(8,128)} %w_in.1, f32[160,1280]{1,0:T(8,128)} %g_in.1, f32[160,1280]{1,0:T(8,128)} %m_in.1, f32[160,1280]{1,0:T(8,128)} %v_in.1, f32[160,320]{1,0:T(8,128)} %l_in.1, ...), custom_call_target="tpu_custom_call" | custom-call | tf_op jit(solution)/shard_map/pallas_call | solution.py:490
  162.4 5.5 %shard_map.120 = (f32[160,1280]{1,0:T(8,128)}, f32[160,1280]{1,0:T(8,128)}, f32[160,1280]{1,0:T(8,128)}, f32[160,320]{1,0:T(8,128)}, f32[640,1280]{1,0:T(8,128)}) custom-call(f32[160,1280]{1,0:T(8,128)} %get-tuple-element.10.refs_0_, f32[160,1280]{1,0:T(8,128)} %get-tuple-element.11.refs_1_, f32[160,1280]{1,0:T(8,128)} %get-tuple-element.12.refs_2_, ...), custom_call_target="tpu_custom_call" | custom-call | tf_op jit(solution)/shard_map/pallas_call | solution.py:500

commit v3 on v2

v3 whole, which is shorter than its diff:
```python
import jax
import jax.numpy as jnp
from jax import lax
from jax.experimental import pallas as pl
from jax.experimental.pallas import tpu as pltpu
from jax.sharding import PartitionSpec as P

BETA1 = 0.9
BETA2 = 0.9
EPS = 1e-8
LR = 0.1
STEP = 10
BIAS_ONE = 1.0 - BETA1 ** STEP
BIAS_TWO = 1.0 - BETA2 ** STEP
MESH = pl.DeviceIdType.MESH
N_REMOTE = 144
N_LOCAL = 16
VMEM_BYTES = 50_000_000
F32 = jnp.float32
BF16 = jnp.bfloat16
SIX_PASSES = ((0, 0), (0, 1), (1, 0), (0, 2), (1, 1), (2, 0))


def dot(a, b, dims=((1,), (0,))):
    return lax.dot_general(a, b, (dims, ((), ())), preferred_element_type=F32)


def split_three(a):
    hi = a.astype(BF16)
    rest = a - hi.astype(F32)
    mid = rest.astype(BF16)
    return hi, mid, (rest - mid.astype(F32)).astype(BF16)


def kernel(w_in, g_in, m_in, v_in, l_in, r_in, ql_in, qr_in, w_out, m_out, v_out, l_out, r_out,
           gf, px, qr, grf, gr, qlf, qlr, qlc, qlt, wx, mx, vx, h, nb, hp, hx, kb, uf, un, uo,
           lc, lf, ln, lhs3, rhs3, la, ss, rs, ls):
    rc, cc = g_in.shape
    cr, hc = 2 * rc, cc // 2
    kk = 2 * cr
    nt = 256 if cc % 256 == 0 else cc
    tb = 128 if kk % 128 == 0 else kk
    row, y = lax.axis_index("row"), lax.axis_index("col")
    x, k = row // 2, row % 2
    d = (y - x + 4) % 4
    rq = cr // 4
    uc, rot = px, grf
    pa = 128 * (hc * 2 // 5 // 128) if hc % 128 == 0 else hc // 2
    pieces = ((0, pa), (pa, hc - pa))

    def ds(start, size, unit=None):
        return pl.ds(start if isinstance(start, int) else pl.multiple_of(start, unit or size), size)

    kcol, ocol = ds(k * hc, hc), ds((1 - k) * hc, hc)
    krow, orow = ds(k * rc, rc), ds((1 - k) * rc, rc)

    counter, pending = [0], []

    def remote(src, dst, dx=0, dk=0, dy=0, index=None, track=True, receive=None):
        if index is None:
            index = counter[0]
            counter[0] += 1
        assert index < N_REMOTE
        copy = pltpu.make_async_remote_copy(
            src_ref=src, dst_ref=dst, send_sem=ss.at[index], recv_sem=rs.at[index if receive is None else receive],
            device_id={"row": ((x + dx + 4) % 4) * 2 + (k + dk) % 2, "col": (y + dy + 4) % 4}, device_id_type=MESH)
        if track:
            pending.append(copy)
        return copy

    lcounter = [0]

    def local(src, dst):
        index = lcounter[0]
        lcounter[0] += 1
        assert index < N_LOCAL
        copy = pltpu.make_async_copy(src, dst, ls.at[index])
        copy.start()
        return copy

    class Ring:
        def __init__(self, buf, at, axis, forward=None, absolute=False):
            def cp(s0, half, s1, step, at=at):
                return remote(buf.at[at(s0, half)], buf.at[at(s0 if absolute else s1, half)], **{axis: step})
            self.ra, self.lb = cp(0, 0, 1, 1), cp(0, 1, 3, -1)
            self.rb, self.la = cp(0, 1, 1, 1), cp(0, 0, 3, -1)
            self.fr, self.fl = [], []
            for part in (forward or [at]):
                self.fr.append(cp(1, 0, 2, 1, part))
                self.fl.append(cp(3, 1, 2, -1, part))

        def own(self):
            for c in (self.ra, self.lb, self.rb, self.la):
                c.start()

        def fwd(self):
            self.ra.wait_recv()
            for c in self.fr:
                c.start()
            self.lb.wait_recv()
            for c in self.fl:
                c.start()

        def near(self):
            self.rb.wait_recv()
            self.la.wait_recv()

        def far(self, parts=None):
            for i in range(len(self.fr)) if parts is None else parts:
                self.fr[i].wait_recv()
                self.fl[i].wait_recv()

    def chunked(total, parts, body):
        size = total // parts

        @pl.loop(0, parts)
        def _(i):
            body(ds(i * size, size), i)

    cp_g = local(g_in, gf.at[krow])
    cp_gk = local(g_in.at[:, kcol], grf.at[krow])
    cp_ql = local(ql_in, qlf.at[krow])
    cp_qr = local(qr_in, r_out)
    cp_own = [local(a.at[:, kcol], b.at[krow]) for a, b in ((m_in, mx), (v_in, vx))] + [local(w_in, wx)]
    cp_l = local(l_in, l_out)
    barrier = pltpu.get_barrier_semaphore()
    for dx, dk, dy in ((1, 0, 0), (-1, 0, 0), (2, 0, 0), (0, 1, 0), (0, 0, 1), (0, 0, -1), (0, 1, 1), (0, 1, -1)):
        pl.semaphore_signal(barrier, inc=1, device_id={"row": ((x + dx + 4) % 4) * 2 + (k + dk) % 2, "col": (y + dy + 4) % 4},
                            device_id_type=MESH)
    pl.semaphore_wait(barrier, 8)

    d_gk = remote(g_in.at[:, ocol], grf.at[krow], dk=1)
    d_g0 = remote(g_in, gf.at[krow], dk=1)
    d_ql = remote(ql_in, qlf.at[krow], dk=1)
    d_own = [remote(a.at[:, ocol], b.at[krow], dk=1) for a, b in ((m_in, mx), (v_in, vx))]
    d_g0.start()
    d_gk.start()
    d_ql.start()

    def grow(s, half):
        return ds((s * 2 + k) * rc + half * (rc // 2), rc // 2)

    def slot_rows(n, start=0, size=None, cols=None):
        size = n if size is None else size
        return lambda s, half: (ds(s * n + start + half * (size // 2), size // 2, 8), slice(None) if cols is None else ds(*cols))

    def whole(s):
        return ds((s * 2 + k) * rc, rc)

    x1 = Ring(gf, grow, "dx")
    x2 = Ring(qr, slot_rows(hc), "dx", [slot_rows(hc, cols=(c * hc + at, n)) for at, n in pieces for c in range(2)])
    x3 = [Ring(h, slot_rows(cr, cols=piece), "dx") for piece in pieces]
    x4 = [Ring(nb, slot_rows(cr, cols=piece), "dx") for piece in pieces]
    y1 = Ring(gr, slot_rows(cr), "dy")
    y2 = Ring(qlr, slot_rows(cr, start=k * rc, size=rc), "dy")
    y3 = Ring(qlc, lambda s, half: (pl.ds(1 + 2 * half, 2 - half), (y - s + 4) % 4), "dy", absolute=True)
    d_g = {s: remote(gf.at[whole(s)], gf.at[whole(s)], dk=1) for s in (1, 3, 2)}

    def prow(s, c):
        return ds((s * 2 + c) * rc, rc)

    p_src, p_fwd, q_src, q_fwd = {}, {}, {}, {}
    for s in (0, 1, 3, 2):
        pi, qi = counter[0], counter[0] + 1
        counter[0] += 2
        p_src[s] = remote(gf.at[prow(s, 0), kcol], px.at[prow(s, 0)], dy=1, index=pi, track=False)
        p_fwd[s] = remote(px.at[prow(s, 0)], px.at[prow(s, 0)], dy=1, index=pi, track=False)
        q_src[s] = remote(gf.at[prow(s, 1), kcol], px.at[prow(s, 1)], dy=-1, index=qi, track=False)
        q_fwd[s] = remote(px.at[prow(s, 1)], px.at[prow(s, 1)], dy=-1, index=qi, track=False)

    def panel_source(s):
        @pl.when(d == 0)
        def _():
            p_src[s].start()
            q_src[s].start()

    def panel_first(s):
        @pl.when(d == 1)
        def _():
            p_fwd[s].wait_recv()
            p_fwd[s].start()

        @pl.when(d == 3)
        def _():
            q_fwd[s].wait_recv()
            q_fwd[s].start()

    def panel_second(s):
        @pl.when(d == 2)
        def _():
            p_fwd[s].wait_recv()
            p_fwd[s].start()
            q_fwd[s].wait_recv()
            q_fwd[s].start()

    def panel_third(s):
        @pl.when(d == 3)
        def _():
            p_fwd[s].wait_recv()

        @pl.when(d == 1)
        def _():
            q_fwd[s].wait_recv()

    def h_part(s, cols):
        t = (d + s) % 4
        part = dot(gr[ds(t * cr, cr), :], qr[ds(s * hc, hc), cols])
        if s == 0:
            hp[:, cols] = part
        else:
            hp[:, cols] += part

    def split_right(p):
        base = p * kk

        def body(r, i):
            for q, piece in enumerate(split_three(gf[ds(base + i * (kk // 8), kk // 8, 8), :])):
                rhs3[ds(q * kk + i * (kk // 8), kk // 8, 8), :] = piece

        chunked(kk, 8, body)
        if p == 0:
            for q in range(3):
                la[ds(q * rc, rc), :] = rhs3[ds(q * kk + k * rc, rc, rc), :]

    def split_left(p):
        base = p * kk

        @pl.when(d == 0)
        def _():
            chunked(kk, 4, lambda r, i: px.__setitem__(
                (ds(base + i * (kk // 4), kk // 4, 8), slice(None)), gf[ds(base + i * (kk // 4), kk // 4, 8), kcol]))

        def body(cols, i):
            for q, piece in enumerate(split_three(px[ds(base + i * tb, tb, 8), :].T)):
                lhs3[ds(q * hc, hc), cols] = piece

        chunked(kk, kk // tb, body)

    def product(p, m):
        def body(cols, i):
            acc = sum(dot(lhs3[ds(a * hc + m * (hc // 2), hc // 2), :], rhs3[ds(b * kk, kk), cols]) for a, b in SIX_PASSES)
            at = (ds(m * (hc // 2), hc // 2), cols)
            if p == 0:
                r_out[at] = BETA2 * r_out[at] + (1.0 - BETA2) * acc
            else:
                r_out[at] += (1.0 - BETA2) * acc

        chunked(cc, cc // nt, body)

    def l_slot(s):
        e = (x - y - s + 8) % 4
        at = [ds(q * kk + (s % 2) * cr, cr) for q in range(3)]
        high = dot(la[...], rhs3[at[0], :], ((1,), (1,)))
        middle = dot(la[ds(0, 2 * rc), :], rhs3[at[1], :], ((1,), (1,)))
        low = dot(la[ds(0, rc), :], rhs3[at[2], :], ((1,), (1,)))
        lc[ds(e * rc, rc), :] = high[:rc] + (high[rc:2 * rc] + middle[:rc]) + (high[2 * rc:] + middle[rc:] + low)

    class Sum:
        def __init__(self, buf, far, near, n, compute):
            self.buf, self.far_, self.near_, self.n, self.compute = buf, far, near, n, compute
            hn = n // 2
            self.rows = lambda e, half: ds(e * n + half * hn, hn)
            rows = self.rows
            self.fa = remote(buf.at[rows(2, 0)], far.at[ds(0, hn)], dy=1)
            self.fb = remote(buf.at[rows(2, 1)], far.at[ds(hn, hn)], dy=-1)
            self.r1b = remote(buf.at[rows(1, 1)], near.at[ds(hn, hn)], dy=1)
            self.l1a = remote(buf.at[rows(3, 0)], near.at[ds(n, hn)], dy=-1)
            self.r1a = remote(buf.at[rows(1, 0)], near.at[ds(0, hn)], dy=1)
            self.l1b = remote(buf.at[rows(3, 1)], near.at[ds(n + hn, hn)], dy=-1)

        def begin(self):
            self.compute(2)
            self.fa.start()
            self.fb.start()
            self.compute(1)
            self.r1b.start()
            self.compute(3)
            self.l1a.start()
            self.compute(0)

        def middle(self):
            hn, buf, far, rows = self.n // 2, self.buf, self.far_, self.rows
            self.fa.wait_recv()
            buf[rows(1, 0), :] += far[ds(0, hn), :]
            self.r1a.start()
            self.fb.wait_recv()
            buf[rows(3, 1), :] += far[ds(hn, hn), :]
            self.l1b.start()

        def finish(self):
            for c in (self.r1b, self.l1a, self.r1a, self.l1b):
                c.wait_recv()

        def total(self, start, size):
            n = self.n
            return self.buf[ds(start, size, 8), :] + (self.near_[ds(start, size, 8), :] + self.near_[ds(n + start, size, 8), :])

    class RowSum(Sum):
        def __init__(self, buf, far, near, n, compute):
            self.buf, self.far_, self.near_, self.n, self.compute = buf, far, near, n, compute
            hn = n // 2
            self.rows = lambda e, half: ds(e * n + half * hn, hn)
            rows = self.rows
            self.fa = remote(buf.at[rows(2, 0)], far.at[ds(0, hn)], dy=1)
            self.fb = remote(buf.at[rows(2, 1)], far.at[ds(hn, hn)], dy=-1)
            base = counter[0]
            counter[0] += 4

            def send(e, half, side):
                return remote(buf.at[rows(e, half)], near.at[ds(side * hn, hn), kcol], dk=half - k + 2, dy=(1, -1)[side],
                              receive=base + side * 2 + k)
            self.r1b, self.r1a = send(1, 1, 0), send(1, 0, 0)
            self.l1a, self.l1b = send(3, 0, 1), send(3, 1, 1)
            self.arrivals = [remote(buf.at[rows(0, 0)], near.at[ds(side * hn, hn), ds(core * hc, hc)], dk=1, index=base + side * 2 + core,
                                    track=False) for side in range(2) for core in range(2)]

        def finish(self):
            for c in self.arrivals:
                c.wait_recv()

    cp_g.wait()
    x1.own()
    d_g0.wait_recv()
    panel_source(0)
    cp_gk.wait()
    d_gk.wait_recv()
    chunked(cr, 4, lambda r, i: gr.__setitem__((r, slice(None)), grf[r, :].astype(BF16)))
    y1.own()
    cp_ql.wait()
    d_ql.wait_recv()
    qlr[ds(0, cr), :] = qlf[...].astype(BF16)
    y2.own()
    for c in d_own:
        c.start()
    cp_qr.wait()
    chunked(hc, 8, lambda r, i: qr.__setitem__((r, slice(None)), r_out[r, :].astype(BF16)))
    cp_r = local(r_in, r_out)
    x1.fwd()
    x2.own()
    panel_first(0)
    y1.fwd()
    y2.fwd()
    x1.near()
    d_g[1].start()
    d_g[3].start()
    d_g[1].wait_recv()
    panel_source(1)
    d_g[3].wait_recv()
    panel_source(3)
    y1.near()
    y1.far()
    h_part(0, ocol)
    h_part(0, kcol)
    x1.far()
    d_g[2].start()
    d_g[2].wait_recv()
    panel_source(2)
    y2.near()
    y2.far()
    d_q = [remote(qlr.at[ds(s * cr + k * rc, rc)], qlr.at[ds(s * cr + k * rc, rc)], dk=1) for s in (1, 3, 2)]
    for c in d_q:
        c.start()
    for c in d_q:
        c.wait_recv()
    qlc[0] = qlr[ds(d * cr, cr), :].reshape(4, rq, qlr.shape[1])
    a2a = []
    for s in (1, 3, 2):
        t = (y - x - s + 8) % 4
        a2a.append(remote(qlr.at[ds(t * cr + y * rq, rq, rq)], qlc.at[s, y], dx=s))
        a2a[-1].start()
    split_right(0)
    panel_first(1)
    panel_second(0)
    panel_first(3)
    panel_second(1)
    panel_third(0)
    x2.fwd()
    panel_first(2)
    panel_second(3)
    panel_third(1)
    cp_r.wait()
    split_left(0)
    product(0, 0)
    product(0, 1)
    x2.near()
    for s in (1, 3):
        h_part(s, ocol)
        h_part(s, kcol)
    for c in a2a:
        c.wait_recv()
    y3.own()

    def columns(core, piece):
        at, n = pieces[piece]
        return ds(core * hc + at, n, 128)

    d_h = [remote(hp.at[:, columns(1 - k, p)], hx.at[:, ds(*pieces[p])], dk=1) for p in range(2)]

    def h_send(p):
        x2.far((2 * p, 2 * p + 1))
        h_part(2, columns(1 - k, p))
        d_h[p].start()
        h_part(2, columns(k, p))

    def h_finish(p):
        d_h[p].wait_recv()
        h[ds(0, cr), ds(*pieces[p])] = (hp[:, columns(k, p)] + hx[:, ds(*pieces[p])]).astype(BF16)
        x3[p].own()

    h_send(0)
    h_finish(0)
    y3.fwd()
    l_slot(0)
    l_slot(1)
    panel_second(2)
    panel_third(3)
    split_right(1)
    h_send(1)
    x3[0].fwd()
    h_finish(1)
    panel_third(2)
    split_left(1)
    product(1, 0)
    y3.near()
    y3.far()
    qlt[...] = qlc[...].reshape(4 * cr, qlc.shape[3]).T
    for c in cp_own:
        c.wait()
    for c in d_own:
        c.wait_recv()
    x3[1].fwd()

    def moments(p):
        x3[p].near()
        x3[p].far()
        cols = ds(*pieces[p])
        rot[:, cols] = dot(qlt[...], h[:, cols])

        def body(r, i):
            rotated = rot[r, cols]
            new_first = BETA1 * mx[r, cols] + (1.0 - BETA1) * rotated
            new_second = BETA2 * vx[r, cols] + (1.0 - BETA2) * rotated * rotated
            mx[r, cols] = new_first
            vx[r, cols] = new_second
            direction = (new_first / BIAS_ONE) / (jnp.sqrt(new_second / BIAS_TWO) + EPS)
            nb[r, cols] = direction.astype(BF16)

        chunked(cr, 10 if cr % 160 == 0 else 1, body)

    moments(0)
    x4[0].own()
    product(1, 1)
    moments(1)
    x4[0].fwd()
    x4[1].own()
    outs = []
    for buf, out in ((mx, m_out), (vx, v_out)):
        outs.append(remote(buf.at[orow], out.at[:, kcol], dk=1))
        outs[-1].start()
        out[:, kcol] = buf[krow, :]
    l_slot(2)
    l_slot(3)
    l_sum = Sum(lc, lf, ln, rc, lambda e: None)
    l_sum.begin()

    d_k = [remote(kb.at[ds(k * cr, cr), ds(*piece)], kb.at[ds(k * cr, cr), ds(*piece)], dk=1) for piece in pieces]

    def k_part(p, slots):
        cols = ds(*pieces[p])
        return sum(dot(qlr[ds(((d + s) % 4) * cr, cr), :], nb[ds(s * cr, cr), cols]) for s in slots)

    def u_part(e, p):
        s = (x - y - e + 8) % 4
        at, n = pieces[p]
        part = sum(dot(kb[ds(c * cr, cr), ds(at, n)], qr[ds(s * hc, hc), ds(c * hc + at, n)], ((1,), (1,))) for c in range(2))
        if p == 0:
            uc[ds(e * cr, cr), :] = part
        else:
            uc[ds(e * cr, cr), :] += part

    x4[0].near()
    x4[0].far()
    kb[ds(k * cr, cr), ds(*pieces[0])] = k_part(0, range(4)).astype(BF16)
    d_k[0].start()
    x4[1].fwd()
    for s in (0, 1, 3, 2):
        @pl.when(d != 3)
        def _():
            p_fwd[s].wait_send()

        @pl.when(d != 1)
        def _():
            q_fwd[s].wait_send()
    d_k[0].wait_recv()
    for e in (2, 1, 3, 0):
        u_part(e, 0)
    x4[1].near()
    rot[:, ds(*pieces[1])] = k_part(1, (0, 1, 3))
    l_sum.middle()
    x4[1].far()
    kb[ds(k * cr, cr), ds(*pieces[1])] = (rot[:, ds(*pieces[1])] + k_part(1, (2,))).astype(BF16)
    d_k[1].start()
    d_k[1].wait_recv()
    u_sum = RowSum(uc, uf, un, cr, lambda e: u_part(e, 1))
    u_sum.begin()
    d_u = remote(uc.at[orow], uo, dk=1)
    d_u.start()
    l_sum.finish()
    cp_l.wait()
    l_out[...] = BETA2 * l_out[...] + (1.0 - BETA2) * l_sum.total(0, rc)
    for c in outs:
        c.wait_recv()
    u_sum.middle()
    d_u.wait_recv()
    u_sum.finish()
    for mine, cols in ((True, kcol), (False, ocol)):
        total = (uc[krow, :] if mine else uo[...]) + (un[ds(0, rc), cols] + un[ds(rc, rc), cols])
        w_out[:, cols] = wx[:, cols] - LR * total
    for c in pending:
        c.wait_send()


def write_kernel(*refs):
    n = (len(refs) - 1) // 2
    copies = [pltpu.make_async_copy(a, b, refs[-1].at[i]) for i, (a, b) in enumerate(zip(refs[:n], refs[n:2 * n]))]
    for c in copies:
        c.start()
    for c in copies:
        c.wait()


def solution(mesh):
    tile_spec = P(("layer", "row"), "col")

    def step(weight, grad_in, mom_first, mom_second, stat_left, stat_right, basis_left, basis_right):
        rc, cc = grad_in.shape
        cr, hc, q = 2 * rc, cc // 2, basis_left.shape[1]
        scratch = [
            ((4 * cr, cc), F32), ((4 * cr, hc), F32), ((4 * hc, cc), BF16),
            ((cr, hc), F32), ((4 * cr, hc), BF16),
            ((cr, q), F32), ((4 * cr, q), BF16), ((4, 4, cr // 4, q), BF16), ((q, 4 * cr), BF16),
            ((rc, cc), F32), ((cr, hc), F32), ((cr, hc), F32),
            ((4 * cr, hc), BF16), ((4 * cr, hc), BF16), ((cr, cc), F32),
            ((cr, hc), F32),
            ((2 * cr, hc), BF16), ((cr, hc), F32), ((cr, cc), F32), ((rc, hc), F32),
            ((4 * rc, q), F32), ((rc, q), F32), ((2 * rc, q), F32),
            ((3 * hc, 2 * cr), BF16), ((6 * cr, cc), BF16), ((3 * rc, cc), BF16),
        ]
        args = (weight, grad_in, mom_first, mom_second, stat_left, stat_right, basis_left, basis_right)
        vmem_spec, any_spec = pl.BlockSpec(memory_space=pltpu.VMEM), pl.BlockSpec(memory_space=pl.ANY)
        outs = tuple(jax.ShapeDtypeStruct(a.shape, F32) for a in (weight, mom_first, mom_second, stat_left, stat_right))
        results = pl.pallas_call(
            kernel,
            out_shape=outs,
            in_specs=[pl.BlockSpec(memory_space=pltpu.HBM)] * 8,
            out_specs=(vmem_spec,) * 5,
            scratch_shapes=[pltpu.VMEM(s, t) for s, t in scratch]
            + [pltpu.SemaphoreType.DMA((N_REMOTE,)), pltpu.SemaphoreType.DMA((N_REMOTE,)), pltpu.SemaphoreType.DMA((N_LOCAL,))],
            compiler_params=pltpu.CompilerParams(collective_id=0, has_side_effects=True, vmem_limit_bytes=VMEM_BYTES),
        )(*(pltpu.with_memory_space_constraint(a, pltpu.HBM) for a in args))
        return pl.pallas_call(
            write_kernel,
            out_shape=outs,
            in_specs=[any_spec] * 5,
            out_specs=(any_spec,) * 5,
            scratch_shapes=[pltpu.SemaphoreType.DMA((5,))],
            compiler_params=pltpu.CompilerParams(vmem_limit_bytes=1_000_000),
        )(*(pltpu.with_memory_space_constraint(a, pltpu.VMEM) for a in results))

    return jax.shard_map(step, mesh=mesh, in_specs=(tile_spec,) * 8, out_specs=(tile_spec,) * 5, check_vma=False)
```

time: 168 us -> 157 us (0.935)
  Pallas kernels: 167 us -> 156 us
    pallas_call x2, Pallas kernels: 167 us -> 156 us  [the longest x1 154 us: step(): pl.pallas_call(kernel, out_shape=outs, in_specs=[pl.BlockSpec(memory_spac...]
where the time goes in v3:
time: 157 us
  Pallas kernels  156 us (99%)
    pallas_call x1, Pallas kernels, step(): pl.pallas_call(kernel, out_shape=outs, in_specs=[pl.BlockSpec(memory_spac...  154 us

profile of v3, /device:TPU:97, one launch (start us, length us, event | category | flops | bytes accessed | tf_op | source)
XLA Modules:
  0.0 157.2 jit_solution(1088992972409977424)
XLA Ops:
  0.6 153.7 %shard_map.119 = (f32[160,1280]{1,0:T(8,128)S(1)}, f32[160,1280]{1,0:T(8,128)S(1)}, f32[160,1280]{1,0:T(8,128)S(1)}, f32[160,320]{1,0:T(8,128)S(1)}, f32[640,1280]{1,0:T(8,128)S(1)}) custom-call(f32[160,1280]{1,0:T(8,128)} %w_in.1, f32[160,1280]{1,0:T(8,128)} %g_in.1, f32[160,1280]{1,0:T(8,128)} %m_in.1, f32[160,1280]{1,0:T(8,128)} %v_in.1, ...), custom_call_target="tpu_custom_call" | custom-call | tf_op jit(solution)/shard_map/pallas_call | solution.py:552
  154.4 2.6 %shard_map.120 = (f32[160,1280]{1,0:T(8,128)}, f32[160,1280]{1,0:T(8,128)}, f32[160,1280]{1,0:T(8,128)}, f32[160,320]{1,0:T(8,128)}, f32[640,1280]{1,0:T(8,128)}) custom-call(f32[160,1280]{1,0:T(8,128)S(1)} %get-tuple-element.10.refs_0_, f32[160,1280]{1,0:T(8,128)S(1)} %get-tuple-element.11.refs_1_, f32[160,1280]{1,0:T(8,128)S(1)} %get-tuple-element.12.refs_2_, ...), custom_call_target="tpu_custom_call" | custom-call | tf_op jit(solution)/shard_map/pallas_call | solution.py:561

commit v4 on v3

--- a/solution.py
+++ b/solution.py
@@ -1,3 +1,5 @@
+import functools
+
 import jax
 import jax.numpy as jnp
 from jax import lax
@@ -13,8 +15,7 @@
 BIAS_ONE = 1.0 - BETA1 ** STEP
 BIAS_TWO = 1.0 - BETA2 ** STEP
 MESH = pl.DeviceIdType.MESH
-N_REMOTE = 144
-N_LOCAL = 16
+N_SEND, N_RECEIVE, N_LOCAL = 33, 71, 9
 VMEM_BYTES = 50_000_000
 F32 = jnp.float32
 BF16 = jnp.bfloat16
@@ -54,19 +55,26 @@
     kcol, ocol = ds(k * hc, hc), ds((1 - k) * hc, hc)
     krow, orow = ds(k * rc, rc), ds((1 - k) * rc, rc)
 
-    counter, pending = [0], []
-
-    def remote(src, dst, dx=0, dk=0, dy=0, index=None, track=True, receive=None):
-        if index is None:
-            index = counter[0]
-            counter[0] += 1
-        assert index < N_REMOTE
+    sends, receives, pending = [0], [0], []
+
+    def new(counter, limit):
+        counter[0] += 1
+        assert counter[0] <= limit
+        return counter[0] - 1
+
+    def remote(src, dst, dx=0, dk=0, dy=0, send=None, receive=None):
+        own = send is None
         copy = pltpu.make_async_remote_copy(
-            src_ref=src, dst_ref=dst, send_sem=ss.at[index], recv_sem=rs.at[index if receive is None else receive],
+            src_ref=src, dst_ref=dst, send_sem=ss.at[new(sends, N_SEND) if own else send],
+            recv_sem=rs.at[new(receives, N_RECEIVE) if receive is None else receive],
             device_id={"row": ((x + dx + 4) % 4) * 2 + (k + dk) % 2, "col": (y + dy + 4) % 4}, device_id_type=MESH)
-        if track:
+        if own:
             pending.append(copy)
         return copy
+
+    def group(ref):
+        send, receive = new(sends, N_SEND), new(receives, N_RECEIVE)
+        return send, receive, remote(ref, ref, dk=1, send=send, receive=receive)
 
     lcounter = [0]
 
@@ -79,15 +87,26 @@
         return copy
 
     class Ring:
-        def __init__(self, buf, at, axis, forward=None, absolute=False):
-            def cp(s0, half, s1, step, at=at):
-                return remote(buf.at[at(s0, half)], buf.at[at(s0 if absolute else s1, half)], **{axis: step})
+        def __init__(self, buf, at, axis, total, near, far, forward=None, absolute=False):
+            send = new(sends, N_SEND)
+            pending.append(remote(buf.at[total], buf.at[total], dk=1, send=send, receive=0))
+
+            def cp(s0, half, s1, step, receive=None, at=at):
+                return remote(buf.at[at(s0, half)], buf.at[at(s0 if absolute else s1, half)], send=send, receive=receive, **{axis: step})
+
+            def wait(view):
+                receive = new(receives, N_RECEIVE)
+                return receive, remote(buf.at[view], buf.at[view], dk=1, send=send, receive=receive)
             self.ra, self.lb = cp(0, 0, 1, 1), cp(0, 1, 3, -1)
-            self.rb, self.la = cp(0, 1, 1, 1), cp(0, 0, 3, -1)
-            self.fr, self.fl = [], []
-            for part in (forward or [at]):
-                self.fr.append(cp(1, 0, 2, 1, part))
-                self.fl.append(cp(3, 1, 2, -1, part))
+            receive, self.near_ = wait(near)
+            self.rb, self.la = cp(0, 1, 1, 1, receive), cp(0, 0, 3, -1, receive)
+            self.fr, self.fl, self.far_ = [], [], []
+            for parts, view in forward or [([at], far)]:
+                receive, wait_far = wait(view)
+                self.far_.append(wait_far)
+                for part in parts:
+                    self.fr.append(cp(1, 0, 2, 1, receive, part))
+                    self.fl.append(cp(3, 1, 2, -1, receive, part))
 
         def own(self):
             for c in (self.ra, self.lb, self.rb, self.la):
@@ -102,13 +121,11 @@
                 c.start()
 
         def near(self):
-            self.rb.wait_recv()
-            self.la.wait_recv()
+            self.near_.wait_recv()
 
         def far(self, parts=None):
-            for i in range(len(self.fr)) if parts is None else parts:
-                self.fr[i].wait_recv()
-                self.fl[i].wait_recv()
+            for i in range(len(self.far_)) if parts is None else parts:
+                self.far_[i].wait_recv()
 
     def chunked(total, parts, body):
         size = total // parts
@@ -132,7 +149,9 @@
     d_gk = remote(g_in.at[:, ocol], grf.at[krow], dk=1)
     d_g0 = remote(g_in, gf.at[krow], dk=1)
     d_ql = remote(ql_in, qlf.at[krow], dk=1)
-    d_own = [remote(a.at[:, ocol], b.at[krow], dk=1) for a, b in ((m_in, mx), (v_in, vx))]
+    own_send, own_receive, d_own_all = group(mx)
+    pending.append(d_own_all)
+    d_own = [remote(a.at[:, ocol], b.at[krow], dk=1, send=own_send, receive=own_receive) for a, b in ((m_in, mx), (v_in, vx))]
     d_g0.start()
     d_gk.start()
     d_ql.start()
@@ -147,26 +166,33 @@
     def whole(s):
         return ds((s * 2 + k) * rc, rc)
 
-    x1 = Ring(gf, grow, "dx")
-    x2 = Ring(qr, slot_rows(hc), "dx", [slot_rows(hc, cols=(c * hc + at, n)) for at, n in pieces for c in range(2)])
-    x3 = [Ring(h, slot_rows(cr, cols=piece), "dx") for piece in pieces]
-    x4 = [Ring(nb, slot_rows(cr, cols=piece), "dx") for piece in pieces]
-    y1 = Ring(gr, slot_rows(cr), "dy")
-    y2 = Ring(qlr, slot_rows(cr, start=k * rc, size=rc), "dy")
-    y3 = Ring(qlc, lambda s, half: (pl.ds(1 + 2 * half, 2 - half), (y - s + 4) % 4), "dy", absolute=True)
+    def tiles(n, cols=None):
+        cols = slice(None) if cols is None else ds(*cols)
+        return {"total": (ds(0, 3 * n), cols), "near": (ds(0, n), cols), "far": (ds(0, n), cols)}
+
+    x1 = Ring(gf, grow, "dx", **tiles(rc))
+    x2 = Ring(qr, slot_rows(hc), "dx", **tiles(hc), forward=[
+        ([slot_rows(hc, cols=(c * hc + at, n)) for c in range(2)], (ds(0, hc), ds(0, 2 * n))) for at, n in pieces])
+    x3 = [Ring(h, slot_rows(cr, cols=piece), "dx", **tiles(cr, piece)) for piece in pieces]
+    x4 = [Ring(nb, slot_rows(cr, cols=piece), "dx", **tiles(cr, piece)) for piece in pieces]
+    y1 = Ring(gr, slot_rows(cr), "dy", **tiles(cr))
+    y2 = Ring(qlr, slot_rows(cr, start=k * rc, size=rc), "dy", **tiles(rc))
+    y3 = Ring(qlc, lambda s, half: (pl.ds(1 + 2 * half, 2 - half), (y - s + 4) % 4), "dy", absolute=True,
+              total=(pl.ds(0, 3), pl.ds(0, 3)), near=(pl.ds(0, 3), 0), far=(pl.ds(0, 3), 0))
     d_g = {s: remote(gf.at[whole(s)], gf.at[whole(s)], dk=1) for s in (1, 3, 2)}
 
     def prow(s, c):
         return ds((s * 2 + c) * rc, rc)
 
     p_src, p_fwd, q_src, q_fwd = {}, {}, {}, {}
+    p_send, q_send = new(sends, N_SEND), new(sends, N_SEND)
+    p_all, q_all = (remote(px.at[ds(0, 4 * rc)], px.at[ds(0, 4 * rc)], dk=1, send=i, receive=0) for i in (p_send, q_send))
     for s in (0, 1, 3, 2):
-        pi, qi = counter[0], counter[0] + 1
-        counter[0] += 2
-        p_src[s] = remote(gf.at[prow(s, 0), kcol], px.at[prow(s, 0)], dy=1, index=pi, track=False)
-        p_fwd[s] = remote(px.at[prow(s, 0)], px.at[prow(s, 0)], dy=1, index=pi, track=False)
-        q_src[s] = remote(gf.at[prow(s, 1), kcol], px.at[prow(s, 1)], dy=-1, index=qi, track=False)
-        q_fwd[s] = remote(px.at[prow(s, 1)], px.at[prow(s, 1)], dy=-1, index=qi, track=False)
+        pi, qi = new(receives, N_RECEIVE), new(receives, N_RECEIVE)
+        p_src[s] = remote(gf.at[prow(s, 0), kcol], px.at[prow(s, 0)], dy=1, send=p_send, receive=pi)
+        p_fwd[s] = remote(px.at[prow(s, 0)], px.at[prow(s, 0)], dy=1, send=p_send, receive=pi)
+        q_src[s] = remote(gf.at[prow(s, 1), kcol], px.at[prow(s, 1)], dy=-1, send=q_send, receive=qi)
+        q_fwd[s] = remote(px.at[prow(s, 1)], px.at[prow(s, 1)], dy=-1, send=q_send, receive=qi)
 
     def panel_source(s):
         @pl.when(d == 0)
@@ -210,6 +236,8 @@
         else:
             hp[:, cols] += part
 
+    units = 2 * (cc // nt)
+
     def split_right(p):
         base = p * kk
 
@@ -236,16 +264,17 @@
 
         chunked(kk, kk // tb, body)
 
-    def product(p, m):
-        def body(cols, i):
+    def product(p, first, last):
+        @pl.loop(first, last)
+        def _(i):
+            m, j = i // (cc // nt), i % (cc // nt)
+            rows = ds(m * (hc // 2), hc // 2)
+            cols = ds(j * nt, nt)
             acc = sum(dot(lhs3[ds(a * hc + m * (hc // 2), hc // 2), :], rhs3[ds(b * kk, kk), cols]) for a, b in SIX_PASSES)
-            at = (ds(m * (hc // 2), hc // 2), cols)
             if p == 0:
-                r_out[at] = BETA2 * r_out[at] + (1.0 - BETA2) * acc
+                r_out[rows, cols] = BETA2 * r_out[rows, cols] + (1.0 - BETA2) * acc
             else:
-                r_out[at] += (1.0 - BETA2) * acc
-
-        chunked(cc, cc // nt, body)
+                r_out[rows, cols] += (1.0 - BETA2) * acc
 
     def l_slot(s):
         e = (x - y - s + 8) % 4
@@ -256,27 +285,27 @@
         lc[ds(e * rc, rc), :] = high[:rc] + (high[rc:2 * rc] + middle[:rc]) + (high[2 * rc:] + middle[rc:] + low)
 
     class Sum:
-        def __init__(self, buf, far, near, n, compute):
-            self.buf, self.far_, self.near_, self.n, self.compute = buf, far, near, n, compute
+        def __init__(self, buf, far, near, n):
+            self.buf, self.far_, self.near_, self.n = buf, far, near, n
             hn = n // 2
             self.rows = lambda e, half: ds(e * n + half * hn, hn)
+            send = new(sends, N_SEND)
+            receive = new(receives, N_RECEIVE)
+            pending.append(remote(buf.at[ds(0, 3 * n)], buf.at[ds(0, 3 * n)], dk=1, send=send, receive=receive))
+            self.arrivals = remote(near, near, dk=1, send=send, receive=receive)
             rows = self.rows
-            self.fa = remote(buf.at[rows(2, 0)], far.at[ds(0, hn)], dy=1)
-            self.fb = remote(buf.at[rows(2, 1)], far.at[ds(hn, hn)], dy=-1)
-            self.r1b = remote(buf.at[rows(1, 1)], near.at[ds(hn, hn)], dy=1)
-            self.l1a = remote(buf.at[rows(3, 0)], near.at[ds(n, hn)], dy=-1)
-            self.r1a = remote(buf.at[rows(1, 0)], near.at[ds(0, hn)], dy=1)
-            self.l1b = remote(buf.at[rows(3, 1)], near.at[ds(n + hn, hn)], dy=-1)
+            self.fa = remote(buf.at[rows(2, 0)], far.at[ds(0, hn)], dy=1, send=send)
+            self.fb = remote(buf.at[rows(2, 1)], far.at[ds(hn, hn)], dy=-1, send=send)
+            self.r1b, self.r1a = self.to(1, 1, 0, send, receive), self.to(1, 0, 0, send, receive)
+            self.l1a, self.l1b = self.to(3, 0, 1, send, receive), self.to(3, 1, 1, send, receive)
+
+        def to(self, e, half, side, send, receive):
+            return remote(self.buf.at[self.rows(e, half)], self.near_.at[ds(side * self.n + half * (self.n // 2), self.n // 2)],
+                          dy=(1, -1)[side], send=send, receive=receive)
 
         def begin(self):
-            self.compute(2)
-            self.fa.start()
-            self.fb.start()
-            self.compute(1)
-            self.r1b.start()
-            self.compute(3)
-            self.l1a.start()
-            self.compute(0)
+            for c in (self.fa, self.fb, self.r1b, self.l1a):
+                c.start()
 
         def middle(self):
             hn, buf, far, rows = self.n // 2, self.buf, self.far_, self.rows
@@ -288,35 +317,17 @@
             self.l1b.start()
 
         def finish(self):
-            for c in (self.r1b, self.l1a, self.r1a, self.l1b):
-                c.wait_recv()
+            self.arrivals.wait_recv()
 
         def total(self, start, size):
             n = self.n
             return self.buf[ds(start, size, 8), :] + (self.near_[ds(start, size, 8), :] + self.near_[ds(n + start, size, 8), :])
 
     class RowSum(Sum):
-        def __init__(self, buf, far, near, n, compute):
-            self.buf, self.far_, self.near_, self.n, self.compute = buf, far, near, n, compute
-            hn = n // 2
-            self.rows = lambda e, half: ds(e * n + half * hn, hn)
-            rows = self.rows
-            self.fa = remote(buf.at[rows(2, 0)], far.at[ds(0, hn)], dy=1)
-            self.fb = remote(buf.at[rows(2, 1)], far.at[ds(hn, hn)], dy=-1)
-            base = counter[0]
-            counter[0] += 4
-
-            def send(e, half, side):
-                return remote(buf.at[rows(e, half)], near.at[ds(side * hn, hn), kcol], dk=half - k + 2, dy=(1, -1)[side],
-                              receive=base + side * 2 + k)
-            self.r1b, self.r1a = send(1, 1, 0), send(1, 0, 0)
-            self.l1a, self.l1b = send(3, 0, 1), send(3, 1, 1)
-            self.arrivals = [remote(buf.at[rows(0, 0)], near.at[ds(side * hn, hn), ds(core * hc, hc)], dk=1, index=base + side * 2 + core,
-                                    track=False) for side in range(2) for core in range(2)]
-
-        def finish(self):
-            for c in self.arrivals:
-                c.wait_recv()
+        def to(self, e, half, side, send, receive):
+            hn = self.n // 2
+            return remote(self.buf.at[self.rows(e, half)], self.near_.at[ds(side * hn, hn), kcol], dk=half - k + 2,
+                          dy=(1, -1)[side], send=send, receive=receive)
 
     cp_g.wait()
     x1.own()
@@ -357,17 +368,25 @@
     panel_source(2)
     y2.near()
     y2.far()
-    d_q = [remote(qlr.at[ds(s * cr + k * rc, rc)], qlr.at[ds(s * cr + k * rc, rc)], dk=1) for s in (1, 3, 2)]
-    for c in d_q:
-        c.start()
-    for c in d_q:
-        c.wait_recv()
+    q_send, q_receive, d_q_all = group(qlr.at[ds(0, 3 * rc)])
+    pending.append(d_q_all)
+    for s in (1, 3, 2):
+        at = ds(s * cr + k * rc, rc)
+        remote(qlr.at[at], qlr.at[at], dk=1, send=q_send, receive=q_receive).start()
+    d_q_all.wait_recv()
     qlc[0] = qlr[ds(d * cr, cr), :].reshape(4, rq, qlr.shape[1])
     a2a = []
-    for s in (1, 3, 2):
+    for s, core in ((1, 0), (3, 1), (2, 0)):
         t = (y - x - s + 8) % 4
-        a2a.append(remote(qlr.at[ds(t * cr + y * rq, rq, rq)], qlc.at[s, y], dx=s))
-        a2a[-1].start()
+        far, near = new(sends, N_SEND), new(sends, N_SEND)
+        a2a.append((core, remote(qlr.at[ds(t * cr + y * rq, rq, rq)], qlc.at[s, y], dx=s, send=far),
+                    remote(qlc.at[s, y], qlc.at[s, y], dk=1, send=near)))
+
+    def quarters(action):
+        for core, across, over in a2a:
+            pl.when(k == core)(functools.partial(action, across, over))
+
+    quarters(lambda across, over: across.start())
     split_right(0)
     panel_first(1)
     panel_second(0)
@@ -380,15 +399,21 @@
     panel_third(1)
     cp_r.wait()
     split_left(0)
-    product(0, 0)
-    product(0, 1)
+    product(0, 0, units)
     x2.near()
     for s in (1, 3):
         h_part(s, ocol)
         h_part(s, kcol)
-    for c in a2a:
-        c.wait_recv()
+    def hand_over(across, over):
+        across.wait_recv()
+        over.start()
+
+    quarters(hand_over)
+    for core, _, over in a2a:
+        pl.when(k != core)(over.wait_recv)
     y3.own()
+    panel_second(2)
+    panel_third(3)
 
     def columns(core, piece):
         at, n = pieces[piece]
@@ -397,7 +422,7 @@
     d_h = [remote(hp.at[:, columns(1 - k, p)], hx.at[:, ds(*pieces[p])], dk=1) for p in range(2)]
 
     def h_send(p):
-        x2.far((2 * p, 2 * p + 1))
+        x2.far((p,))
         h_part(2, columns(1 - k, p))
         d_h[p].start()
         h_part(2, columns(k, p))
@@ -409,26 +434,23 @@
 
     h_send(0)
     h_finish(0)
-    y3.fwd()
     l_slot(0)
     l_slot(1)
-    panel_second(2)
-    panel_third(3)
+    y3.fwd()
     split_right(1)
+    l_slot(2)
+    l_slot(3)
+    l_sum = Sum(lc, lf, ln, rc)
+    l_sum.begin()
     h_send(1)
     x3[0].fwd()
     h_finish(1)
     panel_third(2)
     split_left(1)
-    product(1, 0)
-    y3.near()
-    y3.far()
-    qlt[...] = qlc[...].reshape(4 * cr, qlc.shape[3]).T
+    product(1, 0, units // 5)
     for c in cp_own:
         c.wait()
-    for c in d_own:
-        c.wait_recv()
-    x3[1].fwd()
+    d_own_all.wait_recv()
 
     def moments(p):
         x3[p].near()
@@ -447,21 +469,23 @@
 
         chunked(cr, 10 if cr % 160 == 0 else 1, body)
 
+    y3.near()
+    y3.far()
+    qlt[...] = qlc[...].reshape(4 * cr, qlc.shape[3]).T
     moments(0)
+    x3[1].fwd()
     x4[0].own()
-    product(1, 1)
+    l_sum.middle()
+    product(1, units // 5, units * 3 // 5)
     moments(1)
     x4[0].fwd()
     x4[1].own()
-    outs = []
+    out_send, out_receive, outs_all = group(mx)
+    pending.append(outs_all)
     for buf, out in ((mx, m_out), (vx, v_out)):
-        outs.append(remote(buf.at[orow], out.at[:, kcol], dk=1))
-        outs[-1].start()
+        remote(buf.at[orow], out.at[:, kcol], dk=1, send=out_send, receive=out_receive).start()
         out[:, kcol] = buf[krow, :]
-    l_slot(2)
-    l_slot(3)
-    l_sum = Sum(lc, lf, ln, rc, lambda e: None)
-    l_sum.begin()
+    product(1, units * 3 // 5, units)
 
     d_k = [remote(kb.at[ds(k * cr, cr), ds(*piece)], kb.at[ds(k * cr, cr), ds(*piece)], dk=1) for piece in pieces]
 
@@ -469,47 +493,60 @@
         cols = ds(*pieces[p])
         return sum(dot(qlr[ds(((d + s) % 4) * cr, cr), :], nb[ds(s * cr, cr), cols]) for s in slots)
 
-    def u_part(e, p):
+    def u_part(e, p, core, half=None):
         s = (x - y - e + 8) % 4
         at, n = pieces[p]
-        part = sum(dot(kb[ds(c * cr, cr), ds(at, n)], qr[ds(s * hc, hc), ds(c * hc + at, n)], ((1,), (1,))) for c in range(2))
-        if p == 0:
-            uc[ds(e * cr, cr), :] = part
-        else:
-            uc[ds(e * cr, cr), :] += part
+        start, size = (0, cr) if half is None else (half * rc, rc)
+        part = dot(kb[ds(core * cr + start, size, rc), ds(at, n)], qr[ds(s * hc, hc), ds(core * hc + at, n, 128)], ((1,), (1,)))
+        return ds(e * cr + start, size), part
+
+    def u_add(*which):
+        rows, part = u_part(*which)
+        uc[rows, :] += part
 
     x4[0].near()
     x4[0].far()
     kb[ds(k * cr, cr), ds(*pieces[0])] = k_part(0, range(4)).astype(BF16)
     d_k[0].start()
     x4[1].fwd()
-    for s in (0, 1, 3, 2):
-        @pl.when(d != 3)
-        def _():
-            p_fwd[s].wait_send()
-
-        @pl.when(d != 1)
-        def _():
-            q_fwd[s].wait_send()
+    @pl.when(d != 3)
+    def _():
+        p_all.wait_send()
+
+    @pl.when(d != 1)
+    def _():
+        q_all.wait_send()
+
     d_k[0].wait_recv()
     for e in (2, 1, 3, 0):
-        u_part(e, 0)
+        rows, part = u_part(e, 0, 0)
+        uc[rows, :] = part + u_part(e, 0, 1)[1]
     x4[1].near()
     rot[:, ds(*pieces[1])] = k_part(1, (0, 1, 3))
-    l_sum.middle()
     x4[1].far()
     kb[ds(k * cr, cr), ds(*pieces[1])] = (rot[:, ds(*pieces[1])] + k_part(1, (2,))).astype(BF16)
     d_k[1].start()
+    u_sum = RowSum(uc, uf, un, cr)
+    for e in (2, 1):
+        u_add(e, 1, k)
     d_k[1].wait_recv()
-    u_sum = RowSum(uc, uf, un, cr, lambda e: u_part(e, 1))
-    u_sum.begin()
+    u_add(2, 1, 1 - k, 0)
+    u_sum.fa.start()
+    u_add(2, 1, 1 - k, 1)
+    u_sum.fb.start()
+    u_add(1, 1, 1 - k)
+    u_sum.r1b.start()
+    u_add(3, 1, k)
+    u_add(3, 1, 1 - k)
+    u_sum.l1a.start()
+    u_add(0, 1, k)
+    u_add(0, 1, 1 - k)
     d_u = remote(uc.at[orow], uo, dk=1)
     d_u.start()
     l_sum.finish()
     cp_l.wait()
     l_out[...] = BETA2 * l_out[...] + (1.0 - BETA2) * l_sum.total(0, rc)
-    for c in outs:
-        c.wait_recv()
+    outs_all.wait_recv()
     u_sum.middle()
     d_u.wait_recv()
     u_sum.finish()
@@ -518,11 +555,20 @@
         w_out[:, cols] = wx[:, cols] - LR * total
     for c in pending:
         c.wait_send()
+    for core, across, over in a2a:
+        @pl.when(k == core)
+        def _():
+            across.wait_send()
+            over.wait_send()
 
 
 def write_kernel(*refs):
     n = (len(refs) - 1) // 2
-    copies = [pltpu.make_async_copy(a, b, refs[-1].at[i]) for i, (a, b) in enumerate(zip(refs[:n], refs[n:2 * n]))]
+    copies = []
+    for a, b in zip(refs[:n], refs[n:2 * n]):
+        step = a.shape[0] // 4 if a.shape[0] % 32 == 0 and a.shape[0] > 256 else a.shape[0]
+        for r in range(0, a.shape[0], step):
+            copies.append(pltpu.make_async_copy(a.at[pl.ds(r, step)], b.at[pl.ds(r, step)], refs[-1].at[len(copies)]))
     for c in copies:
         c.start()
     for c in copies:
@@ -555,7 +601,7 @@
             in_specs=[pl.BlockSpec(memory_space=pltpu.HBM)] * 8,
             out_specs=(vmem_spec,) * 5,
             scratch_shapes=[pltpu.VMEM(s, t) for s, t in scratch]
-            + [pltpu.SemaphoreType.DMA((N_REMOTE,)), pltpu.SemaphoreType.DMA((N_REMOTE,)), pltpu.SemaphoreType.DMA((N_LOCAL,))],
+            + [pltpu.SemaphoreType.DMA((n,)) for n in (N_SEND, N_RECEIVE, N_LOCAL)],
             compiler_params=pltpu.CompilerParams(collective_id=0, has_side_effects=True, vmem_limit_bytes=VMEM_BYTES),
         )(*(pltpu.with_memory_space_constraint(a, pltpu.HBM) for a in args))
         return pl.pallas_call(
@@ -563,7 +609,7 @@
             out_shape=outs,
             in_specs=[any_spec] * 5,
             out_specs=(any_spec,) * 5,
-            scratch_shapes=[pltpu.SemaphoreType.DMA((5,))],
+            scratch_shapes=[pltpu.SemaphoreType.DMA((8,))],
             compiler_params=pltpu.CompilerParams(vmem_limit_bytes=1_000_000),
         )(*(pltpu.with_memory_space_constraint(a, pltpu.VMEM) for a in results))
 

time: 157 us -> 152 us (0.968)
  Pallas kernels: 156 us -> 151 us
    pallas_call x1, Pallas kernels: 154 us -> 148 us  [step(): pl.pallas_call(kernel, out_shape=outs, in_specs=[pl.BlockSpec(memory_spac...]
where the time goes in v4:
time: 152 us
  Pallas kernels  151 us (99%)
    pallas_call x1, Pallas kernels, step(): pl.pallas_call(kernel, out_shape=outs, in_specs=[pl.BlockSpec(memory_spac...  148 us

profile of v4, /device:TPU:97, one launch (start us, length us, event | category | flops | bytes accessed | tf_op | source)
XLA Modules:
  0.0 151.8 jit_solution(18104464618669661470)
XLA Ops:
  0.6 148.3 %shard_map.119 = (f32[160,1280]{1,0:T(8,128)S(1)}, f32[160,1280]{1,0:T(8,128)S(1)}, f32[160,1280]{1,0:T(8,128)S(1)}, f32[160,320]{1,0:T(8,128)S(1)}, f32[640,1280]{1,0:T(8,128)S(1)}) custom-call(f32[160,1280]{1,0:T(8,128)} %w_in.1, f32[160,1280]{1,0:T(8,128)} %g_in.1, f32[160,1280]{1,0:T(8,128)} %m_in.1, f32[160,1280]{1,0:T(8,128)} %v_in.1, ...), custom_call_target="tpu_custom_call" | custom-call | tf_op jit(solution)/shard_map/pallas_call | solution.py:598
  149.0 2.6 %shard_map.120 = (f32[160,1280]{1,0:T(8,128)}, f32[160,1280]{1,0:T(8,128)}, f32[160,1280]{1,0:T(8,128)}, f32[160,320]{1,0:T(8,128)}, f32[640,1280]{1,0:T(8,128)}) custom-call(f32[160,1280]{1,0:T(8,128)S(1)} %get-tuple-element.10.refs_0_, f32[160,1280]{1,0:T(8,128)S(1)} %get-tuple-element.11.refs_1_, f32[160,1280]{1,0:T(8,128)S(1)} %get-tuple-element.12.refs_2_, ...), custom_call_target="tpu_custom_call" | custom-call | tf_op jit(solution)/shard_map/pallas_call | solution.py:607

commit v5 on v4

--- a/solution.py
+++ b/solution.py
@@ -15,14 +15,16 @@
 BIAS_ONE = 1.0 - BETA1 ** STEP
 BIAS_TWO = 1.0 - BETA2 ** STEP
 MESH = pl.DeviceIdType.MESH
+OTHERS = (1, 3, 2)
 N_SEND, N_RECEIVE, N_LOCAL = 33, 71, 9
 VMEM_BYTES = 50_000_000
 F32 = jnp.float32
 BF16 = jnp.bfloat16
-SIX_PASSES = ((0, 0), (0, 1), (1, 0), (0, 2), (1, 1), (2, 0))
-
-
-def dot(a, b, dims=((1,), (0,))):
+SIX_PASSES = [(a, b) for a in range(3) for b in range(3 - a)]
+NN, NT = (((1,), (i,)) for i in range(2))
+
+
+def dot(a, b, dims=NN):
     return lax.dot_general(a, b, (dims, ((), ())), preferred_element_type=F32)
 
 
@@ -62,12 +64,15 @@
         assert counter[0] <= limit
         return counter[0] - 1
 
+    def device(dx=0, dk=0, dy=0):
+        return {"row": ((x + dx + 4) % 4) * 2 + (k + dk) % 2, "col": (y + dy + 4) % 4}
+
     def remote(src, dst, dx=0, dk=0, dy=0, send=None, receive=None):
         own = send is None
         copy = pltpu.make_async_remote_copy(
             src_ref=src, dst_ref=dst, send_sem=ss.at[new(sends, N_SEND) if own else send],
             recv_sem=rs.at[new(receives, N_RECEIVE) if receive is None else receive],
-            device_id={"row": ((x + dx + 4) % 4) * 2 + (k + dk) % 2, "col": (y + dy + 4) % 4}, device_id_type=MESH)
+            device_id=device(dx, dk, dy), device_id_type=MESH)
         if own:
             pending.append(copy)
         return copy
@@ -141,10 +146,12 @@
     cp_own = [local(a.at[:, kcol], b.at[krow]) for a, b in ((m_in, mx), (v_in, vx))] + [local(w_in, wx)]
     cp_l = local(l_in, l_out)
     barrier = pltpu.get_barrier_semaphore()
-    for dx, dk, dy in ((1, 0, 0), (-1, 0, 0), (2, 0, 0), (0, 1, 0), (0, 0, 1), (0, 0, -1), (0, 1, 1), (0, 1, -1)):
-        pl.semaphore_signal(barrier, inc=1, device_id={"row": ((x + dx + 4) % 4) * 2 + (k + dk) % 2, "col": (y + dy + 4) % 4},
-                            device_id_type=MESH)
-    pl.semaphore_wait(barrier, 8)
+    partners = [device(dx=2), device(dk=1)]
+    for step in (1, -1):
+        partners += [device(dx=step), device(dy=step), device(dk=1, dy=step)]
+    for partner in partners:
+        pl.semaphore_signal(barrier, inc=1, device_id=partner, device_id_type=MESH)
+    pl.semaphore_wait(barrier, len(partners))
 
     d_gk = remote(g_in.at[:, ocol], grf.at[krow], dk=1)
     d_g0 = remote(g_in, gf.at[krow], dk=1)
@@ -177,9 +184,10 @@
     x4 = [Ring(nb, slot_rows(cr, cols=piece), "dx", **tiles(cr, piece)) for piece in pieces]
     y1 = Ring(gr, slot_rows(cr), "dy", **tiles(cr))
     y2 = Ring(qlr, slot_rows(cr, start=k * rc, size=rc), "dy", **tiles(rc))
+    three = pl.ds(0, 3)
     y3 = Ring(qlc, lambda s, half: (pl.ds(1 + 2 * half, 2 - half), (y - s + 4) % 4), "dy", absolute=True,
-              total=(pl.ds(0, 3), pl.ds(0, 3)), near=(pl.ds(0, 3), 0), far=(pl.ds(0, 3), 0))
-    d_g = {s: remote(gf.at[whole(s)], gf.at[whole(s)], dk=1) for s in (1, 3, 2)}
+              total=(three, three), near=(three, 0), far=(three, 0))
+    d_g = {s: remote(gf.at[whole(s)], gf.at[whole(s)], dk=1) for s in OTHERS}
 
     def prow(s, c):
         return ds((s * 2 + c) * rc, rc)
@@ -187,7 +195,7 @@
     p_src, p_fwd, q_src, q_fwd = {}, {}, {}, {}
     p_send, q_send = new(sends, N_SEND), new(sends, N_SEND)
     p_all, q_all = (remote(px.at[ds(0, 4 * rc)], px.at[ds(0, 4 * rc)], dk=1, send=i, receive=0) for i in (p_send, q_send))
-    for s in (0, 1, 3, 2):
+    for s in (0, *OTHERS):
         pi, qi = new(receives, N_RECEIVE), new(receives, N_RECEIVE)
         p_src[s] = remote(gf.at[prow(s, 0), kcol], px.at[prow(s, 0)], dy=1, send=p_send, receive=pi)
         p_fwd[s] = remote(px.at[prow(s, 0)], px.at[prow(s, 0)], dy=1, send=p_send, receive=pi)
@@ -279,9 +287,9 @@
     def l_slot(s):
         e = (x - y - s + 8) % 4
         at = [ds(q * kk + (s % 2) * cr, cr) for q in range(3)]
-        high = dot(la[...], rhs3[at[0], :], ((1,), (1,)))
-        middle = dot(la[ds(0, 2 * rc), :], rhs3[at[1], :], ((1,), (1,)))
-        low = dot(la[ds(0, rc), :], rhs3[at[2], :], ((1,), (1,)))
+        high = dot(la[...], rhs3[at[0], :], NT)
+        middle = dot(la[ds(0, 2 * rc), :], rhs3[at[1], :], NT)
+        low = dot(la[ds(0, rc), :], rhs3[at[2], :], NT)
         lc[ds(e * rc, rc), :] = high[:rc] + (high[rc:2 * rc] + middle[:rc]) + (high[2 * rc:] + middle[rc:] + low)
 
     class Sum:
@@ -370,7 +378,7 @@
     y2.far()
     q_send, q_receive, d_q_all = group(qlr.at[ds(0, 3 * rc)])
     pending.append(d_q_all)
-    for s in (1, 3, 2):
+    for s in OTHERS:
         at = ds(s * cr + k * rc, rc)
         remote(qlr.at[at], qlr.at[at], dk=1, send=q_send, receive=q_receive).start()
     d_q_all.wait_recv()
@@ -497,7 +505,7 @@
         s = (x - y - e + 8) % 4
         at, n = pieces[p]
         start, size = (0, cr) if half is None else (half * rc, rc)
-        part = dot(kb[ds(core * cr + start, size, rc), ds(at, n)], qr[ds(s * hc, hc), ds(core * hc + at, n, 128)], ((1,), (1,)))
+        part = dot(kb[ds(core * cr + start, size, rc), ds(at, n)], qr[ds(s * hc, hc), ds(core * hc + at, n, 128)], NT)
         return ds(e * cr + start, size), part
 
     def u_add(*which):
@@ -564,11 +572,7 @@
 
 def write_kernel(*refs):
     n = (len(refs) - 1) // 2
-    copies = []
-    for a, b in zip(refs[:n], refs[n:2 * n]):
-        step = a.shape[0] // 4 if a.shape[0] % 32 == 0 and a.shape[0] > 256 else a.shape[0]
-        for r in range(0, a.shape[0], step):
-            copies.append(pltpu.make_async_copy(a.at[pl.ds(r, step)], b.at[pl.ds(r, step)], refs[-1].at[len(copies)]))
+    copies = [pltpu.make_async_copy(a, b, refs[-1].at[i]) for i, (a, b) in enumerate(zip(refs, refs[n:-1]))]
     for c in copies:
         c.start()
     for c in copies:
@@ -609,7 +613,7 @@
             out_shape=outs,
             in_specs=[any_spec] * 5,
             out_specs=(any_spec,) * 5,
-            scratch_shapes=[pltpu.SemaphoreType.DMA((8,))],
+            scratch_shapes=[pltpu.SemaphoreType.DMA((len(outs),))],
             compiler_params=pltpu.CompilerParams(vmem_limit_bytes=1_000_000),
         )(*(pltpu.with_memory_space_constraint(a, pltpu.VMEM) for a in results))
 

time: 152 us -> 152 us (level)
  no operation moved by 1% of the time
where the time goes in v5:
time: 152 us
  Pallas kernels  151 us (99%)
    pallas_call x1, Pallas kernels, step(): pl.pallas_call(kernel, out_shape=outs, in_specs=[pl.BlockSpec(memory_spac...  148 us

profile of v5, /device:TPU:97, one launch (start us, length us, event | category | flops | bytes accessed | tf_op | source)
XLA Modules:
  0.0 151.8 jit_solution(13926100389133615502)
XLA Ops:
  0.6 148.4 %shard_map.119 = (f32[160,1280]{1,0:T(8,128)S(1)}, f32[160,1280]{1,0:T(8,128)S(1)}, f32[160,1280]{1,0:T(8,128)S(1)}, f32[160,320]{1,0:T(8,128)S(1)}, f32[640,1280]{1,0:T(8,128)S(1)}) custom-call(f32[160,1280]{1,0:T(8,128)} %w_in.1, f32[160,1280]{1,0:T(8,128)} %g_in.1, f32[160,1280]{1,0:T(8,128)} %m_in.1, f32[160,1280]{1,0:T(8,128)} %v_in.1, ...), custom_call_target="tpu_custom_call" | custom-call | tf_op jit(solution)/shard_map/pallas_call | solution.py:602
  149.0 2.6 %shard_map.120 = (f32[160,1280]{1,0:T(8,128)}, f32[160,1280]{1,0:T(8,128)}, f32[160,1280]{1,0:T(8,128)}, f32[160,320]{1,0:T(8,128)}, f32[640,1280]{1,0:T(8,128)}) custom-call(f32[160,1280]{1,0:T(8,128)S(1)} %get-tuple-element.10.refs_0_, f32[160,1280]{1,0:T(8,128)S(1)} %get-tuple-element.11.refs_1_, f32[160,1280]{1,0:T(8,128)S(1)} %get-tuple-element.12.refs_2_, ...), custom_call_target="tpu_custom_call" | custom-call | tf_op jit(solution)/shard_map/pallas_call | solution.py:611

commit v6 on v5

--- a/solution.py
+++ b/solution.py
@@ -1,4 +1,4 @@
-import functools
+import math
 
 import jax
 import jax.numpy as jnp
@@ -16,7 +16,7 @@
 BIAS_TWO = 1.0 - BETA2 ** STEP
 MESH = pl.DeviceIdType.MESH
 OTHERS = (1, 3, 2)
-N_SEND, N_RECEIVE, N_LOCAL = 33, 71, 9
+N_SEND, N_RECEIVE, N_LOCAL = 13, 51, 7
 VMEM_BYTES = 50_000_000
 F32 = jnp.float32
 BF16 = jnp.bfloat16
@@ -67,62 +67,76 @@
     def device(dx=0, dk=0, dy=0):
         return {"row": ((x + dx + 4) % 4) * 2 + (k + dk) % 2, "col": (y + dy + 4) % 4}
 
+    class Batch:
+        def __init__(self):
+            self.semaphore, self.bytes = new(sends, N_SEND), 0
+
+        def wait(self):
+            rows, rest = divmod(self.bytes, cc * gf.dtype.itemsize)
+            assert rest == 0 and rows <= gf.shape[0]
+            arrival(gf.at[ds(0, rows)], None, self.semaphore).wait_send()
+
     def remote(src, dst, dx=0, dk=0, dy=0, send=None, receive=None):
-        own = send is None
+        if isinstance(send, Batch):
+            send.bytes += math.prod(src.shape) * jnp.dtype(src.dtype).itemsize
+            index = send.semaphore
+        else:
+            index = new(sends, N_SEND) if send is None else send
         copy = pltpu.make_async_remote_copy(
-            src_ref=src, dst_ref=dst, send_sem=ss.at[new(sends, N_SEND) if own else send],
+            src_ref=src, dst_ref=dst, send_sem=ss.at[index],
             recv_sem=rs.at[new(receives, N_RECEIVE) if receive is None else receive],
             device_id=device(dx, dk, dy), device_id_type=MESH)
-        if own:
+        if send is None:
             pending.append(copy)
         return copy
 
-    def group(ref):
-        send, receive = new(sends, N_SEND), new(receives, N_RECEIVE)
-        return send, receive, remote(ref, ref, dk=1, send=send, receive=receive)
-
+    def arrival(view, receive, send=0):
+        return remote(view, view, dk=1, send=send, receive=receive or 0)
+
+    def group(view):
+        receive = new(receives, N_RECEIVE)
+        return receive, arrival(view, receive)
+
+    batch_x, batch_xy, batch_first, batch_last = (Batch() for _ in range(4))
     lcounter = [0]
 
-    def local(src, dst):
-        index = lcounter[0]
-        lcounter[0] += 1
+    def local(src, dst, index=None):
+        if index is None:
+            index = lcounter[0]
+            lcounter[0] += 1
         assert index < N_LOCAL
         copy = pltpu.make_async_copy(src, dst, ls.at[index])
         copy.start()
         return copy
 
     class Ring:
-        def __init__(self, buf, at, axis, total, near, far, forward=None, absolute=False):
-            send = new(sends, N_SEND)
-            pending.append(remote(buf.at[total], buf.at[total], dk=1, send=send, receive=0))
-
-            def cp(s0, half, s1, step, receive=None, at=at):
-                return remote(buf.at[at(s0, half)], buf.at[at(s0 if absolute else s1, half)], send=send, receive=receive, **{axis: step})
-
-            def wait(view):
-                receive = new(receives, N_RECEIVE)
-                return receive, remote(buf.at[view], buf.at[view], dk=1, send=send, receive=receive)
-            self.ra, self.lb = cp(0, 0, 1, 1), cp(0, 1, 3, -1)
-            receive, self.near_ = wait(near)
-            self.rb, self.la = cp(0, 1, 1, 1, receive), cp(0, 0, 3, -1, receive)
+        def __init__(self, buf, at, axis, near, rest, total=None, batch=None, forward=None, absolute=False, joined=False):
+            if batch is None:
+                batch = new(sends, N_SEND)
+                pending.append(arrival(buf.at[total], None, batch))
+
+            def cp(s0, half, s1, step, receive, at=at):
+                return remote(buf.at[at(s0, half)], buf.at[at(s0 if absolute else s1, half)], send=batch, receive=receive, **{axis: step})
+
+            first, self.first = group(buf.at[near])
+            self.ra, self.lb = cp(0, 0, 1, 1, first), cp(0, 1, 3, -1, first)
+            second, self.near_ = group(buf.at[rest if joined else near])
+            self.rb, self.la = cp(0, 1, 1, 1, second), cp(0, 0, 3, -1, second)
             self.fr, self.fl, self.far_ = [], [], []
-            for parts, view in forward or [([at], far)]:
-                receive, wait_far = wait(view)
-                self.far_.append(wait_far)
+            for parts, view in forward or [([at], near)]:
+                last, wait = (second, self.near_) if joined else group(buf.at[view])
+                self.far_.append(wait)
                 for part in parts:
-                    self.fr.append(cp(1, 0, 2, 1, receive, part))
-                    self.fl.append(cp(3, 1, 2, -1, receive, part))
+                    self.fr.append(cp(1, 0, 2, 1, last, part))
+                    self.fl.append(cp(3, 1, 2, -1, last, part))
 
         def own(self):
             for c in (self.ra, self.lb, self.rb, self.la):
                 c.start()
 
         def fwd(self):
-            self.ra.wait_recv()
-            for c in self.fr:
-                c.start()
-            self.lb.wait_recv()
-            for c in self.fl:
+            self.first.wait_recv()
+            for c in self.fr + self.fl:
                 c.start()
 
         def near(self):
@@ -143,8 +157,12 @@
     cp_gk = local(g_in.at[:, kcol], grf.at[krow])
     cp_ql = local(ql_in, qlf.at[krow])
     cp_qr = local(qr_in, r_out)
-    cp_own = [local(a.at[:, kcol], b.at[krow]) for a, b in ((m_in, mx), (v_in, vx))] + [local(w_in, wx)]
     cp_l = local(l_in, l_out)
+    local(w_in, wx, lcounter[0])
+    for a, b in ((m_in, mx), (v_in, vx)):
+        local(a.at[:, kcol], b.at[krow], lcounter[0])
+    cp_own = pltpu.make_async_copy(gf.at[ds(0, cr)], gf.at[ds(0, cr)], ls.at[lcounter[0]])
+    lcounter[0] += 1
     barrier = pltpu.get_barrier_semaphore()
     partners = [device(dx=2), device(dk=1)]
     for step in (1, -1):
@@ -153,12 +171,11 @@
         pl.semaphore_signal(barrier, inc=1, device_id=partner, device_id_type=MESH)
     pl.semaphore_wait(barrier, len(partners))
 
-    d_gk = remote(g_in.at[:, ocol], grf.at[krow], dk=1)
-    d_g0 = remote(g_in, gf.at[krow], dk=1)
+    d_gk = remote(g_in.at[:, ocol], grf.at[krow], dk=1, send=batch_first)
+    d_g0 = remote(g_in, gf.at[krow], dk=1, send=batch_first)
     d_ql = remote(ql_in, qlf.at[krow], dk=1)
-    own_send, own_receive, d_own_all = group(mx)
-    pending.append(d_own_all)
-    d_own = [remote(a.at[:, ocol], b.at[krow], dk=1, send=own_send, receive=own_receive) for a, b in ((m_in, mx), (v_in, vx))]
+    own_receive, d_own_all = group(mx)
+    d_own = [remote(a.at[:, ocol], b.at[krow], dk=1, send=batch_first, receive=own_receive) for a, b in ((m_in, mx), (v_in, vx))]
     d_g0.start()
     d_gk.start()
     d_ql.start()
@@ -175,26 +192,27 @@
 
     def tiles(n, cols=None):
         cols = slice(None) if cols is None else ds(*cols)
-        return {"total": (ds(0, 3 * n), cols), "near": (ds(0, n), cols), "far": (ds(0, n), cols)}
-
-    x1 = Ring(gf, grow, "dx", **tiles(rc))
-    x2 = Ring(qr, slot_rows(hc), "dx", **tiles(hc), forward=[
+        return {"near": (ds(0, n), cols), "rest": (ds(0, 2 * n), cols)}
+
+    x1 = Ring(gf, grow, "dx", **tiles(rc), batch=batch_xy)
+    x2 = Ring(qr, slot_rows(hc), "dx", **tiles(hc), batch=batch_x, forward=[
         ([slot_rows(hc, cols=(c * hc + at, n)) for c in range(2)], (ds(0, hc), ds(0, 2 * n))) for at, n in pieces])
-    x3 = [Ring(h, slot_rows(cr, cols=piece), "dx", **tiles(cr, piece)) for piece in pieces]
-    x4 = [Ring(nb, slot_rows(cr, cols=piece), "dx", **tiles(cr, piece)) for piece in pieces]
-    y1 = Ring(gr, slot_rows(cr), "dy", **tiles(cr))
-    y2 = Ring(qlr, slot_rows(cr, start=k * rc, size=rc), "dy", **tiles(rc))
+    x3 = [Ring(h, slot_rows(cr, cols=piece), "dx", **tiles(cr, piece), batch=batch_x, joined=True) for piece in pieces]
+    x4 = [Ring(nb, slot_rows(cr, cols=piece), "dx", **tiles(cr, piece), batch=batch_xy, joined=p == 0) for p, piece in enumerate(pieces)]
+    y1 = Ring(gr, slot_rows(cr), "dy", **tiles(cr), batch=batch_xy, joined=True)
+    y2 = Ring(qlr, slot_rows(cr, start=k * rc, size=rc), "dy", **tiles(rc), total=ds(0, 3 * rc), joined=True)
     three = pl.ds(0, 3)
     y3 = Ring(qlc, lambda s, half: (pl.ds(1 + 2 * half, 2 - half), (y - s + 4) % 4), "dy", absolute=True,
-              total=(three, three), near=(three, 0), far=(three, 0))
-    d_g = {s: remote(gf.at[whole(s)], gf.at[whole(s)], dk=1) for s in OTHERS}
+              near=(three, 0), rest=(three, pl.ds(0, 2)), total=(three, three), joined=True)
+    near_receive, d_g_near = group(gf.at[ds(0, cr)])
+    d_g = {s: remote(gf.at[whole(s)], gf.at[whole(s)], dk=1, send=batch_first, receive=None if s == 2 else near_receive) for s in OTHERS}
 
     def prow(s, c):
         return ds((s * 2 + c) * rc, rc)
 
     p_src, p_fwd, q_src, q_fwd = {}, {}, {}, {}
     p_send, q_send = new(sends, N_SEND), new(sends, N_SEND)
-    p_all, q_all = (remote(px.at[ds(0, 4 * rc)], px.at[ds(0, 4 * rc)], dk=1, send=i, receive=0) for i in (p_send, q_send))
+    p_all, q_all = (arrival(px.at[ds(0, 4 * rc)], None, i) for i in (p_send, q_send))
     for s in (0, *OTHERS):
         pi, qi = new(receives, N_RECEIVE), new(receives, N_RECEIVE)
         p_src[s] = remote(gf.at[prow(s, 0), kcol], px.at[prow(s, 0)], dy=1, send=p_send, receive=pi)
@@ -293,14 +311,14 @@
         lc[ds(e * rc, rc), :] = high[:rc] + (high[rc:2 * rc] + middle[:rc]) + (high[2 * rc:] + middle[rc:] + low)
 
     class Sum:
-        def __init__(self, buf, far, near, n):
+        def __init__(self, buf, far, near, n, send=None):
             self.buf, self.far_, self.near_, self.n = buf, far, near, n
             hn = n // 2
             self.rows = lambda e, half: ds(e * n + half * hn, hn)
-            send = new(sends, N_SEND)
-            receive = new(receives, N_RECEIVE)
-            pending.append(remote(buf.at[ds(0, 3 * n)], buf.at[ds(0, 3 * n)], dk=1, send=send, receive=receive))
-            self.arrivals = remote(near, near, dk=1, send=send, receive=receive)
+            if send is None:
+                send = new(sends, N_SEND)
+                pending.append(arrival(buf.at[ds(0, 3 * n)], None, send))
+            receive, self.arrivals = group(near)
             rows = self.rows
             self.fa = remote(buf.at[rows(2, 0)], far.at[ds(0, hn)], dy=1, send=send)
             self.fb = remote(buf.at[rows(2, 1)], far.at[ds(hn, hn)], dy=-1, send=send)
@@ -362,11 +380,9 @@
     x1.near()
     d_g[1].start()
     d_g[3].start()
-    d_g[1].wait_recv()
+    d_g_near.wait_recv()
     panel_source(1)
-    d_g[3].wait_recv()
     panel_source(3)
-    y1.near()
     y1.far()
     h_part(0, ocol)
     h_part(0, kcol)
@@ -374,27 +390,30 @@
     d_g[2].start()
     d_g[2].wait_recv()
     panel_source(2)
-    y2.near()
     y2.far()
-    q_send, q_receive, d_q_all = group(qlr.at[ds(0, 3 * rc)])
-    pending.append(d_q_all)
+    q_receive, d_q_all = group(qlr.at[ds(0, 3 * rc)])
+    q_send = new(sends, N_SEND)
+    pending.append(arrival(qlr.at[ds(0, 3 * rc)], None, q_send))
     for s in OTHERS:
         at = ds(s * cr + k * rc, rc)
         remote(qlr.at[at], qlr.at[at], dk=1, send=q_send, receive=q_receive).start()
     d_q_all.wait_recv()
     qlc[0] = qlr[ds(d * cr, cr), :].reshape(4, rq, qlr.shape[1])
-    a2a = []
-    for s, core in ((1, 0), (3, 1), (2, 0)):
+    across_receive, across_all = group(qlc.at[three, 0])
+    across_send = new(sends, N_SEND)
+    across = []
+    for s in OTHERS:
         t = (y - x - s + 8) % 4
-        far, near = new(sends, N_SEND), new(sends, N_SEND)
-        a2a.append((core, remote(qlr.at[ds(t * cr + y * rq, rq, rq)], qlc.at[s, y], dx=s, send=far),
-                    remote(qlc.at[s, y], qlc.at[s, y], dk=1, send=near)))
-
-    def quarters(action):
-        for core, across, over in a2a:
-            pl.when(k == core)(functools.partial(action, across, over))
-
-    quarters(lambda across, over: across.start())
+        across.append(remote(qlr.at[ds(t * cr + y * rq, rq, rq)], qlc.at[s, y], dx=s, send=across_send, receive=across_receive))
+    over_send = new(sends, N_SEND)
+    over = remote(qlc.at[pl.ds(1, 3), y], qlc.at[pl.ds(1, 3), y], dk=1, send=over_send)
+    sent = [arrival(qlc.at[three, 0], None, across_send), over]
+
+    @pl.when(k == 1)
+    def _():
+        for c in across:
+            c.start()
+
     split_right(0)
     panel_first(1)
     panel_second(0)
@@ -412,13 +431,12 @@
     for s in (1, 3):
         h_part(s, ocol)
         h_part(s, kcol)
-    def hand_over(across, over):
-        across.wait_recv()
+    @pl.when(k == 1)
+    def _():
+        across_all.wait_recv()
         over.start()
 
-    quarters(hand_over)
-    for core, _, over in a2a:
-        pl.when(k != core)(over.wait_recv)
+    pl.when(k == 0)(over.wait_recv)
     y3.own()
     panel_second(2)
     panel_third(3)
@@ -427,7 +445,7 @@
         at, n = pieces[piece]
         return ds(core * hc + at, n, 128)
 
-    d_h = [remote(hp.at[:, columns(1 - k, p)], hx.at[:, ds(*pieces[p])], dk=1) for p in range(2)]
+    d_h = [remote(hp.at[:, columns(1 - k, p)], hx.at[:, ds(*pieces[p])], dk=1, send=batch_first) for p in range(2)]
 
     def h_send(p):
         x2.far((p,))
@@ -456,12 +474,10 @@
     panel_third(2)
     split_left(1)
     product(1, 0, units // 5)
-    for c in cp_own:
-        c.wait()
+    cp_own.wait()
     d_own_all.wait_recv()
 
     def moments(p):
-        x3[p].near()
         x3[p].far()
         cols = ds(*pieces[p])
         rot[:, cols] = dot(qlt[...], h[:, cols])
@@ -477,7 +493,6 @@
 
         chunked(cr, 10 if cr % 160 == 0 else 1, body)
 
-    y3.near()
     y3.far()
     qlt[...] = qlc[...].reshape(4 * cr, qlc.shape[3]).T
     moments(0)
@@ -488,14 +503,13 @@
     moments(1)
     x4[0].fwd()
     x4[1].own()
-    out_send, out_receive, outs_all = group(mx)
-    pending.append(outs_all)
+    out_receive, outs_all = group(mx)
     for buf, out in ((mx, m_out), (vx, v_out)):
-        remote(buf.at[orow], out.at[:, kcol], dk=1, send=out_send, receive=out_receive).start()
+        remote(buf.at[orow], out.at[:, kcol], dk=1, send=batch_last, receive=out_receive).start()
         out[:, kcol] = buf[krow, :]
     product(1, units * 3 // 5, units)
 
-    d_k = [remote(kb.at[ds(k * cr, cr), ds(*piece)], kb.at[ds(k * cr, cr), ds(*piece)], dk=1) for piece in pieces]
+    d_k = [remote(kb.at[ds(k * cr, cr), ds(*piece)], kb.at[ds(k * cr, cr), ds(*piece)], dk=1, send=batch_last) for piece in pieces]
 
     def k_part(p, slots):
         cols = ds(*pieces[p])
@@ -512,7 +526,6 @@
         rows, part = u_part(*which)
         uc[rows, :] += part
 
-    x4[0].near()
     x4[0].far()
     kb[ds(k * cr, cr), ds(*pieces[0])] = k_part(0, range(4)).astype(BF16)
     d_k[0].start()
@@ -534,7 +547,7 @@
     x4[1].far()
     kb[ds(k * cr, cr), ds(*pieces[1])] = (rot[:, ds(*pieces[1])] + k_part(1, (2,))).astype(BF16)
     d_k[1].start()
-    u_sum = RowSum(uc, uf, un, cr)
+    u_sum = RowSum(uc, uf, un, cr, batch_last)
     for e in (2, 1):
         u_add(e, 1, k)
     d_k[1].wait_recv()
@@ -549,7 +562,7 @@
     u_sum.l1a.start()
     u_add(0, 1, k)
     u_add(0, 1, 1 - k)
-    d_u = remote(uc.at[orow], uo, dk=1)
+    d_u = remote(uc.at[orow], uo, dk=1, send=batch_last)
     d_u.start()
     l_sum.finish()
     cp_l.wait()
@@ -563,11 +576,13 @@
         w_out[:, cols] = wx[:, cols] - LR * total
     for c in pending:
         c.wait_send()
-    for core, across, over in a2a:
-        @pl.when(k == core)
-        def _():
-            across.wait_send()
-            over.wait_send()
+    for batch in (batch_x, batch_xy, batch_first, batch_last):
+        batch.wait()
+
+    @pl.when(k == 1)
+    def _():
+        for c in sent:
+            c.wait_send()
 
 
 def write_kernel(*refs):

time: 152 us -> 152 us (level)
  no operation moved by 1% of the time
where the time goes in v6:
time: 152 us
  Pallas kernels  151 us (99%)
    pallas_call x1, Pallas kernels, step(): pl.pallas_call(kernel, out_shape=outs, in_specs=[pl.BlockSpec(memory_spac...  149 us

profile of v6, /device:TPU:97, one launch (start us, length us, event | category | flops | bytes accessed | tf_op | source)
XLA Modules:
  0.0 152.0 jit_solution(1898923148304850058)
XLA Ops:
  0.6 148.5 %shard_map.119 = (f32[160,1280]{1,0:T(8,128)S(1)}, f32[160,1280]{1,0:T(8,128)S(1)}, f32[160,1280]{1,0:T(8,128)S(1)}, f32[160,320]{1,0:T(8,128)S(1)}, f32[640,1280]{1,0:T(8,128)S(1)}) custom-call(f32[160,1280]{1,0:T(8,128)} %w_in.1, f32[160,1280]{1,0:T(8,128)} %g_in.1, f32[160,1280]{1,0:T(8,128)} %m_in.1, f32[160,1280]{1,0:T(8,128)} %v_in.1, ...), custom_call_target="tpu_custom_call" | custom-call | tf_op jit(solution)/shard_map/pallas_call | solution.py:617
  149.2 2.6 %shard_map.120 = (f32[160,1280]{1,0:T(8,128)}, f32[160,1280]{1,0:T(8,128)}, f32[160,1280]{1,0:T(8,128)}, f32[160,320]{1,0:T(8,128)}, f32[640,1280]{1,0:T(8,128)}) custom-call(f32[160,1280]{1,0:T(8,128)S(1)} %get-tuple-element.10.refs_0_, f32[160,1280]{1,0:T(8,128)S(1)} %get-tuple-element.11.refs_1_, f32[160,1280]{1,0:T(8,128)S(1)} %get-tuple-element.12.refs_2_, ...), custom_call_target="tpu_custom_call" | custom-call | tf_op jit(solution)/shard_map/pallas_call | solution.py:626

commit v7 on v6

--- a/solution.py
+++ b/solution.py
@@ -16,7 +16,7 @@
 BIAS_TWO = 1.0 - BETA2 ** STEP
 MESH = pl.DeviceIdType.MESH
 OTHERS = (1, 3, 2)
-N_SEND, N_RECEIVE, N_LOCAL = 13, 51, 7
+N_SEND, N_RECEIVE, N_LOCAL = 13, 60, 7
 VMEM_BYTES = 50_000_000
 F32 = jnp.float32
 BF16 = jnp.bfloat16
@@ -118,8 +118,7 @@
             def cp(s0, half, s1, step, receive, at=at):
                 return remote(buf.at[at(s0, half)], buf.at[at(s0 if absolute else s1, half)], send=batch, receive=receive, **{axis: step})
 
-            first, self.first = group(buf.at[near])
-            self.ra, self.lb = cp(0, 0, 1, 1, first), cp(0, 1, 3, -1, first)
+            self.ra, self.lb = cp(0, 0, 1, 1, None), cp(0, 1, 3, -1, None)
             second, self.near_ = group(buf.at[rest if joined else near])
             self.rb, self.la = cp(0, 1, 1, 1, second), cp(0, 0, 3, -1, second)
             self.fr, self.fl, self.far_ = [], [], []
@@ -135,9 +134,10 @@
                 c.start()
 
         def fwd(self):
-            self.first.wait_recv()
-            for c in self.fr + self.fl:
-                c.start()
+            for first, parts in ((self.ra, self.fr), (self.lb, self.fl)):
+                first.wait_recv()
+                for c in parts:
+                    c.start()
 
         def near(self):
             self.near_.wait_recv()

time: 152 us -> 151 us (level)
  no operation moved by 1% of the time
where the time goes in v7:
time: 151 us
  Pallas kernels  150 us (99%)
    pallas_call x1, Pallas kernels, step(): pl.pallas_call(kernel, out_shape=outs, in_specs=[pl.BlockSpec(memory_spac...  148 us

profile of v7, /device:TPU:97, one launch (start us, length us, event | category | flops | bytes accessed | tf_op | source)
XLA Modules:
  0.0 151.2 jit_solution(14697486916798831766)
XLA Ops:
  0.6 147.8 %shard_map.119 = (f32[160,1280]{1,0:T(8,128)S(1)}, f32[160,1280]{1,0:T(8,128)S(1)}, f32[160,1280]{1,0:T(8,128)S(1)}, f32[160,320]{1,0:T(8,128)S(1)}, f32[640,1280]{1,0:T(8,128)S(1)}) custom-call(f32[160,1280]{1,0:T(8,128)} %w_in.1, f32[160,1280]{1,0:T(8,128)} %g_in.1, f32[160,1280]{1,0:T(8,128)} %m_in.1, f32[160,1280]{1,0:T(8,128)} %v_in.1, ...), custom_call_target="tpu_custom_call" | custom-call | tf_op jit(solution)/shard_map/pallas_call | solution.py:617
  148.4 2.6 %shard_map.120 = (f32[160,1280]{1,0:T(8,128)}, f32[160,1280]{1,0:T(8,128)}, f32[160,1280]{1,0:T(8,128)}, f32[160,320]{1,0:T(8,128)}, f32[640,1280]{1,0:T(8,128)}) custom-call(f32[160,1280]{1,0:T(8,128)S(1)} %get-tuple-element.10.refs_0_, f32[160,1280]{1,0:T(8,128)S(1)} %get-tuple-element.11.refs_1_, f32[160,1280]{1,0:T(8,128)S(1)} %get-tuple-element.12.refs_2_, ...), custom_call_target="tpu_custom_call" | custom-call | tf_op jit(solution)/shard_map/pallas_call | solution.py:626

commit v8 on v7

--- a/solution.py
+++ b/solution.py
@@ -16,7 +16,7 @@
 BIAS_TWO = 1.0 - BETA2 ** STEP
 MESH = pl.DeviceIdType.MESH
 OTHERS = (1, 3, 2)
-N_SEND, N_RECEIVE, N_LOCAL = 13, 60, 7
+N_SEND, N_RECEIVE, N_LOCAL = 13, 61, 7
 VMEM_BYTES = 50_000_000
 F32 = jnp.float32
 BF16 = jnp.bfloat16
@@ -509,7 +509,10 @@
         out[:, kcol] = buf[krow, :]
     product(1, units * 3 // 5, units)
 
-    d_k = [remote(kb.at[ds(k * cr, cr), ds(*piece)], kb.at[ds(k * cr, cr), ds(*piece)], dk=1, send=batch_last) for piece in pieces]
+    first, last = (ds(*piece) for piece in pieces)
+    d_k = remote(kb.at[ds(k * cr, cr), first], kb.at[ds(k * cr, cr), first], dk=1, send=batch_last)
+    halves = [(ds(half * rc, rc), ds(k * cr + half * rc, rc), ds((d + 2) % 4 * cr + half * rc, rc)) for half in range(2)]
+    d_kb = [remote(kb.at[at, last], kb.at[at, last], dk=1, send=batch_last) for _, at, _ in halves]
 
     def k_part(p, slots):
         cols = ds(*pieces[p])
@@ -528,7 +531,7 @@
 
     x4[0].far()
     kb[ds(k * cr, cr), ds(*pieces[0])] = k_part(0, range(4)).astype(BF16)
-    d_k[0].start()
+    d_k.start()
     x4[1].fwd()
     @pl.when(d != 3)
     def _():
@@ -538,21 +541,23 @@
     def _():
         q_all.wait_send()
 
-    d_k[0].wait_recv()
+    d_k.wait_recv()
     for e in (2, 1, 3, 0):
         rows, part = u_part(e, 0, 0)
         uc[rows, :] = part + u_part(e, 0, 1)[1]
     x4[1].near()
     rot[:, ds(*pieces[1])] = k_part(1, (0, 1, 3))
     x4[1].far()
-    kb[ds(k * cr, cr), ds(*pieces[1])] = (rot[:, ds(*pieces[1])] + k_part(1, (2,))).astype(BF16)
-    d_k[1].start()
+    for (rows, at, left), c in zip(halves, d_kb):
+        kb[at, last] = (rot[rows, last] + dot(qlr[left, :], nb[ds(2 * cr, cr), last])).astype(BF16)
+        c.start()
     u_sum = RowSum(uc, uf, un, cr, batch_last)
     for e in (2, 1):
         u_add(e, 1, k)
-    d_k[1].wait_recv()
+    d_kb[0].wait_recv()
     u_add(2, 1, 1 - k, 0)
     u_sum.fa.start()
+    d_kb[1].wait_recv()
     u_add(2, 1, 1 - k, 1)
     u_sum.fb.start()
     u_add(1, 1, 1 - k)

time: 151 us -> 151 us (level)
  no operation moved by 1% of the time
where the time goes in v8:
time: 151 us
  Pallas kernels  150 us (99%)
    pallas_call x1, Pallas kernels, step(): pl.pallas_call(kernel, out_shape=outs, in_specs=[pl.BlockSpec(memory_spac...  148 us

profile of v8, /device:TPU:97, one launch (start us, length us, event | category | flops | bytes accessed | tf_op | source)
XLA Modules:
  0.0 151.0 jit_solution(9944875427211768386)
XLA Ops:
  0.6 147.5 %shard_map.119 = (f32[160,1280]{1,0:T(8,128)S(1)}, f32[160,1280]{1,0:T(8,128)S(1)}, f32[160,1280]{1,0:T(8,128)S(1)}, f32[160,320]{1,0:T(8,128)S(1)}, f32[640,1280]{1,0:T(8,128)S(1)}) custom-call(f32[160,1280]{1,0:T(8,128)} %w_in.1, f32[160,1280]{1,0:T(8,128)} %g_in.1, f32[160,1280]{1,0:T(8,128)} %m_in.1, f32[160,1280]{1,0:T(8,128)} %v_in.1, ...), custom_call_target="tpu_custom_call" | custom-call | tf_op jit(solution)/shard_map/pallas_call | solution.py:622
  148.2 2.6 %shard_map.120 = (f32[160,1280]{1,0:T(8,128)}, f32[160,1280]{1,0:T(8,128)}, f32[160,1280]{1,0:T(8,128)}, f32[160,320]{1,0:T(8,128)}, f32[640,1280]{1,0:T(8,128)}) custom-call(f32[160,1280]{1,0:T(8,128)S(1)} %get-tuple-element.10.refs_0_, f32[160,1280]{1,0:T(8,128)S(1)} %get-tuple-element.11.refs_1_, f32[160,1280]{1,0:T(8,128)S(1)} %get-tuple-element.12.refs_2_, ...), custom_call_target="tpu_custom_call" | custom-call | tf_op jit(solution)/shard_map/pallas_call | solution.py:631
